TPU v7x, 256 devices: a 4x2x16 block of a 4x16x16 slice. The times are simulated.
256 devices in a mesh: groups: 2 (over y), context: 128 (over x, z, core).
Axes of the slice: x: 4, y: 2, z: 16, core: 2. Of those that a mesh axis runs over, the one named last changes fastest.
The devices are a block of a 4x16x16 slice.
Arguments:
- query_proj: bfloat16 [32768, 5120], P(('groups', 'context')), parts along dimension 0, may hold values from -100 to 100
- key_proj: bfloat16 [32768, 1024], P(('groups', 'context')), parts along dimension 0, may hold values from -100 to 100
- values: bfloat16 [32768, 1024], P(('groups', 'context')), parts along dimension 0, may hold values from -6 to 6
- grad_out: bfloat16 [32768, 5120], P(('groups', 'context')), parts along dimension 0, may hold values from -6 to 6
- query_gain: float32 [5120], replicated, may hold values from 0.1 to 1.9
- key_gain: float32 [1024], replicated, may hold values from 0.1 to 1.9
- segments: int32 [32768], P('groups'), parts along dimension 0, may hold values from 0 to 63, never falling along the last dimension, each value on 1 to 512 neighbouring positions
- layout: int32 [512], P('groups'), parts along dimension 0, may hold values from 0 to 255, as said below
Outputs:
- query_grad: bfloat16 [32768, 5120], P(('groups', 'context')), parts along dimension 0
- key_grad: bfloat16 [32768, 1024], P(('groups', 'context')), parts along dimension 0
- value_grad: bfloat16 [32768, 1024], P(('groups', 'context')), parts along dimension 0
- query_gain_grad: float32 [10240], P('groups'), parts along dimension 0
- key_gain_grad: float32 [2048], P('groups'), parts along dimension 0
There are 2 independent parts, one for each index of `groups`. A program takes and returns all parts, laid end to end along the dimension named above; an argument that names none is the same for every part. Nothing has to cross between parts.
Inputs may be any that keep to these rules, and one draw needn't show every extreme that they name: layout is a permutation of the spans; slots are ordered device by device, 2 to a device, and each aligned run of 8 slots holds the spans of one sequence of 512 positions in some order. `segments`: document numbers never fall along the stream; a document has 1 to 512 positions, and one has exactly 512.
All inputs are finite; a program needn't handle non-finite values.
Results may differ from a plain program's by a relative error of at most 0.0086.
Values may be sent and summed in bfloat16 or wider, within the bound.
A program may use at most 128 MiB of HBM per device.

v0:
```python
import jax
import jax.numpy as jnp
from jax import lax
from jax.sharding import Mesh
from jax.sharding import PartitionSpec as P

QUERY_HEADS = 40
KEY_VALUE_HEADS = 8
HEAD_SIZE = 128
SPAN = 64
SEQ_BITS = 2
SEQ_DEVS = 4
LENGTH = 512
CONTEXT = ("context_0", "context_1", "context_2")
GROUPS_CONTEXT = ("groups", "context_0", "context_1", "context_2")


NORM_EPS = 1e-06
ROPE_BASE = 500000.0


def swapped(block, axis, apart):
    count = lax.axis_size(axis)
    route = []
    for low in range(count):
        high = low | 1 << apart
        if high != low and high < count:
            route += [(low, high), (high, low)]
    return lax.ppermute(block, axis, route)


def for_sending(array):

    def short(part):
        return part.astype(jnp.bfloat16) if part.dtype == jnp.float32 else part

    return jax.tree.map(short, array)


def by_axis(array, axes):
    for axis in axes:
        array = lax.psum(array, axis)
    return array


def rope_angles(positions, head_dim):
    half_dim = head_dim // 2
    inv_freq = jnp.power(ROPE_BASE, -2.0 * jnp.arange(half_dim, dtype=jnp.float32) / head_dim)
    angles = positions.astype(jnp.float32)[:, None] * inv_freq[None, :]
    return (jnp.cos(angles), jnp.sin(angles))


def rotate(inputs, cosine, sine, sign_flip):
    tok_rows = inputs.shape[0]
    half_dim = cosine.shape[1]
    halves = inputs.reshape(tok_rows, inputs.shape[1] // (2 * half_dim), 2, half_dim)
    lower_half = halves[:, :, 0]
    upper_half = halves[:, :, 1]
    cosine_b = cosine[:, None, :]
    sine_b = sine[:, None, :] * sign_flip
    rotated = jnp.stack(
        [lower_half * cosine_b - upper_half * sine_b, upper_half * cosine_b + lower_half * sine_b],
        axis=2,
    )
    return rotated.reshape(tok_rows, inputs.shape[1])


def norm_forward(inputs, gain_row):
    mean_sq = jnp.mean(inputs * inputs, axis=1, keepdims=True)
    factor = lax.rsqrt(mean_sq + NORM_EPS)
    return (inputs * factor * gain_row[None, :], factor)


def norm_backward(inputs, factor, gain_row, upstream):
    weighted = upstream * gain_row[None, :]
    inner_sum = jnp.mean(weighted * inputs, axis=1, keepdims=True)
    grad_in = factor * weighted - inputs * factor * factor * factor * inner_sum
    return (grad_in, jnp.sum(upstream * inputs * factor, axis=0))


def head_gradients(queries, key_rows, value_rows, grad_rows, allowed, query_head_group, head_dim):
    tok_rows = queries.shape[0]
    factor = head_dim ** (-0.5)
    query_heads = queries.reshape(tok_rows, query_head_group, head_dim)
    grad_heads = grad_rows.reshape(tok_rows, query_head_group, head_dim)
    scores = (
        jnp.einsum("qgd,kd->gqk", query_heads, key_rows, preferred_element_type=jnp.float32)
        * factor
    )
    scores = jnp.where(allowed[None], scores, -jnp.inf)
    row_max = jnp.max(scores, axis=2, keepdims=True)
    expo = jnp.exp(scores - row_max)
    attn_probs = expo / jnp.sum(expo, axis=2, keepdims=True)
    dprobs = jnp.einsum("qgd,kd->gqk", grad_heads, value_rows, preferred_element_type=jnp.float32)
    row_delta = jnp.sum(attn_probs * dprobs, axis=2, keepdims=True)
    dscores = (attn_probs * (dprobs - row_delta)).astype(jnp.bfloat16)
    probs_low = attn_probs.astype(jnp.bfloat16)
    query_part = (
        jnp.einsum("gqk,kd->qgd", dscores, key_rows, preferred_element_type=jnp.float32) * factor
    )
    key_part = (
        jnp.einsum("gqk,qgd->kd", dscores, query_heads, preferred_element_type=jnp.float32) * factor
    )
    value_part = jnp.einsum(
        "gqk,qgd->kd", probs_low, grad_heads, preferred_element_type=jnp.float32
    )
    return (query_part.reshape(tok_rows, query_head_group * head_dim), key_part, value_part)


def token_info(devices, tok_rows, layout, segments):
    local_index = jnp.arange(tok_rows, dtype=jnp.int32)
    slot_ids = devices[:, None] * (tok_rows // SPAN) + local_index[None, :] // SPAN
    positions = jnp.take(layout, slot_ids) * SPAN + local_index[None, :] % SPAN
    positions = positions.reshape(-1)
    return (positions, jnp.take(segments, positions))


def body(query_proj, key_proj, values, grad_out, query_gain, key_gain, segments, layout):
    tok_rows = query_proj.shape[0]
    my_index = lax.axis_index(CONTEXT)
    query_head_group = QUERY_HEADS // KEY_VALUE_HEADS
    group_width = query_head_group * HEAD_SIZE
    local_rank = my_index % SEQ_DEVS
    seq_base = my_index - local_rank
    positions, doc_query = token_info(jnp.reshape(my_index, (1,)), tok_rows, layout, segments)
    cosine, sine = rope_angles(positions % LENGTH, HEAD_SIZE)
    q_inputs = query_proj.astype(jnp.float32)
    k_inputs = key_proj.astype(jnp.float32)
    q_normed, q_factor = norm_forward(q_inputs, query_gain)
    k_normed, k_factor = norm_forward(k_inputs, key_gain)
    q_rope = rotate(q_normed, cosine, sine, 1.0).astype(jnp.bfloat16)
    k_rope = rotate(k_normed, cosine, sine, 1.0).astype(jnp.bfloat16)
    bit_order = list(range(SEQ_BITS))
    held_k, held_v = (k_rope, values)
    owners = jnp.reshape(local_rank, (1,))
    for bit in bit_order:
        got_k, got_v = swapped((held_k, held_v), CONTEXT, bit)
        held_k = jnp.concatenate([held_k, got_k], axis=0)
        held_v = jnp.concatenate([held_v, got_v], axis=0)
        owners = jnp.concatenate([owners, jnp.bitwise_xor(owners, 1 << bit)])
    pos_key, doc_key = token_info(seq_base + owners, tok_rows, layout, segments)
    allowed = (doc_key[None, :] == doc_query[:, None]) & (pos_key[None, :] <= positions[:, None])
    query_parts, key_parts, value_parts = ([], [], [])
    for key_value_head in range(KEY_VALUE_HEADS):
        query_part, key_part, value_part = head_gradients(
            q_rope[:, key_value_head * group_width : (key_value_head + 1) * group_width],
            held_k[:, key_value_head * HEAD_SIZE : (key_value_head + 1) * HEAD_SIZE],
            held_v[:, key_value_head * HEAD_SIZE : (key_value_head + 1) * HEAD_SIZE],
            grad_out[:, key_value_head * group_width : (key_value_head + 1) * group_width],
            allowed,
            query_head_group,
            HEAD_SIZE,
        )
        query_parts.append(query_part)
        key_parts.append(key_part)
        value_parts.append(value_part)
    dq_rope = jnp.concatenate(query_parts, axis=1)
    dk_all = jnp.concatenate(key_parts, axis=1)
    dv_all = jnp.concatenate(value_parts, axis=1)
    dq_normed = rotate(dq_rope, cosine, sine, -1.0)
    query_grad, q_gain_part = norm_backward(q_inputs, q_factor, query_gain, dq_normed)
    for bit in reversed(bit_order):
        half_rows = dk_all.shape[0] // 2
        back_k, back_v = swapped(
            (for_sending(dk_all[half_rows:]), for_sending(dv_all[half_rows:])), CONTEXT, bit
        )
        dk_all = dk_all[:half_rows] + back_k
        dv_all = dv_all[:half_rows] + back_v
    dk_normed = rotate(dk_all, cosine, sine, -1.0)
    key_grad, k_gain_part = norm_backward(k_inputs, k_factor, key_gain, dk_normed)
    q_gain_total, k_gain_total = (by_axis(q_gain_part, CONTEXT), by_axis(k_gain_part, CONTEXT))
    return (
        query_grad.astype(jnp.bfloat16),
        key_grad.astype(jnp.bfloat16),
        dv_all.astype(jnp.bfloat16),
        q_gain_total,
        k_gain_total,
    )


def solution(mesh):
    split = Mesh(
        mesh.devices.reshape(mesh.shape["groups"], 4, 16, 2),
        ("groups", "context_0", "context_1", "context_2"),
    )
    placed = (
        P(GROUPS_CONTEXT, None),
        P(GROUPS_CONTEXT, None),
        P(GROUPS_CONTEXT, None),
        P(GROUPS_CONTEXT, None),
        P(),
        P(),
        P("groups"),
        P("groups"),
    )
    return jax.shard_map(
        body,
        mesh=split,
        in_specs=placed,
        out_specs=(
            P(GROUPS_CONTEXT, None),
            P(GROUPS_CONTEXT, None),
            P(GROUPS_CONTEXT, None),
            P("groups"),
            P("groups"),
        ),
        check_vma=False,
    )
```

profile of v0, /device:TPU:33, one launch (start us, length us, event | category | flops | bytes accessed | tf_op | source)
XLA Modules:
  0.0 238.2 jit_solution(13967253927241340696)
XLA Ops:
  1.4 3.5 %gather_fusion.1 = s32[512]{0:T(512)S(1)} fusion(s32[256]{0:T(256)S(1)} %copy-done.2, s32[1024]{0:T(1024)S(1)} %pad_clamp_fusion.2), kind=kCustom, calls=%fused_computation.1 | custom fusion | bytes 6144 | tf_op jit(solution)/shard_map/jit(_take)/gather | solution.py:113
  4.9 1.3 gather_fusion
  6.3 1.1 gather_fusion.3
  9.1 20.5 %collective-permute-start = (bf16[128,1024]{1,0:T(8,128)(2,1)S(1)}, bf16[128,1024]{1,0:T(8,128)(2,1)}, u32[]{:S(2)}, u32[]{:S(2)}) collective-permute-start(bf16[128,1024]{1,0:T(8,128)(2,1)S(1)} %copy.74), channel_id=1, source_target_pairs={{0,1},{1,0},{2,3},{3,2},{4,5},{5,4},{6,7},{7,6},{8,9},{9,8},{10,11... | collective-permute-start | bytes 786440 | tf_op jit(solution)/shard_map/ppermute | solution.py:29
  30.0 3.1 %gather_fusion.2 = s32[512]{0:T(512)S(1)} fusion(s32[16384]{0:T(1024)S(1)} %copy-done, s32[1024]{0:T(1024)S(1)} %get-tuple-element.89), kind=kCustom, calls=%fused_computation.2 | custom fusion | bytes 6144 | tf_op jit(solution)/shard_map/jit(_take)/gather | solution.py:115
  34.8 2.2 fusion.9
  38.3 1.2 copy-done.13
  39.5 1.1 fusion.131
  40.5 1.8 pad_maximum_fusion.3
  43.0 1.7 copy.190
  44.7 1.7 copy.191
  46.4 1.1 fusion.130
  47.5 1.9 pad_maximum_fusion.4
  49.4 1.5 collective-permute-start.3
  50.9 1.7 copy.192
  56.7 1.7 constant_dynamic-update-slice_fusion.1
  58.4 1.2 pad_maximum_fusion.2
  59.6 1.6 fusion.132
  61.2 6.0 %collective-permute-done.3 = bf16[256,1024]{1,0:T(8,128)(2,1)} collective-permute-done((bf16[256,1024]{1,0:T(8,128)(2,1)}, bf16[256,1024]{1,0:T(8,128)(2,1)}, u32[]{:S(2)}, u32[]{:S(2)}) %collective-permute-start.3) | collective-permute-done | bytes 524320 | tf_op jit(solution)/shard_map/ppermute | solution.py:29
  67.2 1.9 constant_dynamic-update-slice_fusion
  69.0 1.8 multiply_reduce_fusion.7
  72.4 2.5 %fusion.57 = f32[512,1024]{0,1:T(8,128)} fusion(bf16[128,5,128]{0,2,1:T(8,128)(2,1)} %bitcast.579, f32[5,128]{1,0:T(8,128)S(1)} %get-tuple-element.56, bf16[128,5,128]{0,2,1:T(8,128)(2,1)S(1)} %bitcast.564, pred[128,512]{0,1:T(8,128)(4,1)S(1)} %copy-done.54, bf16[512,1024]{1,0:T(8,128)(2,1)S(1)} %pad_maximum_fusion.2), kind=kOutput, calls=%fused_computation.120 | convolution fusion | flops 169411712 | bytes 790528 | tf_op jit(solution)/shard_map/gqk,qgd->kd/dot_general | solution.py:104
  74.9 1.6 fusion.133
  76.5 1.8 multiply_reduce_fusion.6
  79.2 1.0 fusion.71
  80.3 2.5 %fusion.134 = (f32[5,128]{1,0:T(8,128)S(1)}, f32[5,128,512]{1,2,0:T(8,128)}) fusion(bf16[128,5,128]{0,2,1:T(8,128)(2,1)} %bitcast.556, pred[128,512]{0,1:T(8,128)(4,1)S(1)} %copy-done.54, bf16[512,1024]{1,0:T(8,128)(2,1)S(1)} %pad_maximum_fusion.2), kind=kOutput, calls=%fused_computation.312 | convolution fusion | flops 85197312 | bytes 1673728 | tf_op jit(solution)/shard_map/sub | solution.py:92
  82.8 1.9 multiply_reduce_fusion.5
  86.9 2.5 %fusion.135 = (f32[5,128]{1,0:T(8,128)S(1)}, f32[5,128,512]{1,2,0:T(8,128)}) fusion(bf16[128,5,128]{0,2,1:T(8,128)(2,1)} %bitcast.553, pred[128,512]{0,1:T(8,128)(4,1)S(1)} %copy-done.54, bf16[512,1024]{1,0:T(8,128)(2,1)S(1)} %pad_maximum_fusion.2), kind=kOutput, calls=%fused_computation.313 | convolution fusion | flops 85197312 | bytes 1673728 | tf_op jit(solution)/shard_map/sub | solution.py:92
  89.4 1.9 multiply_reduce_fusion.4
  92.6 1.1 fusion.67
  93.6 2.5 %fusion.136 = (f32[5,128]{1,0:T(8,128)S(1)}, f32[5,128,512]{1,2,0:T(8,128)}) fusion(bf16[128,5,128]{0,2,1:T(8,128)(2,1)} %bitcast.550, pred[128,512]{0,1:T(8,128)(4,1)S(1)} %copy-done.54, bf16[512,1024]{1,0:T(8,128)(2,1)S(1)} %pad_maximum_fusion.2), kind=kOutput, calls=%fused_computation.314 | convolution fusion | flops 85197312 | bytes 1673728 | tf_op jit(solution)/shard_map/sub | solution.py:92
  96.1 1.9 multiply_reduce_fusion.3
  99.3 1.1 fusion.65
  100.3 2.5 %fusion.137 = (f32[5,128]{1,0:T(8,128)S(1)}, f32[5,128,512]{1,2,0:T(8,128)}) fusion(bf16[128,5,128]{0,2,1:T(8,128)(2,1)} %bitcast.547, pred[128,512]{0,1:T(8,128)(4,1)S(1)} %copy-done.54, bf16[512,1024]{1,0:T(8,128)(2,1)S(1)} %pad_maximum_fusion.2), kind=kOutput, calls=%fused_computation.315 | convolution fusion | flops 85197312 | bytes 1673728 | tf_op jit(solution)/shard_map/sub | solution.py:92
  102.8 1.9 multiply_reduce_fusion.2
  104.9 1.1 convolution_multiply_fusion.10
  106.0 1.1 fusion.63
  107.1 2.5 %fusion.138 = (f32[5,128]{1,0:T(8,128)S(1)}, f32[5,128,512]{1,2,0:T(8,128)}) fusion(bf16[128,5,128]{0,2,1:T(8,128)(2,1)} %bitcast.544, pred[128,512]{0,1:T(8,128)(4,1)S(1)} %copy-done.54, bf16[512,1024]{1,0:T(8,128)(2,1)S(1)} %pad_maximum_fusion.2), kind=kOutput, calls=%fused_computation.316 | convolution fusion | flops 85197312 | bytes 1673728 | tf_op jit(solution)/shard_map/sub | solution.py:92
  109.6 1.9 multiply_reduce_fusion.1
  111.7 1.1 convolution_multiply_fusion.9
  113.8 2.5 %fusion.139 = (f32[5,128]{1,0:T(8,128)S(1)}, f32[5,128,512]{1,2,0:T(8,128)}) fusion(bf16[128,5,128]{0,2,1:T(8,128)(2,1)} %bitcast.541, pred[128,512]{0,1:T(8,128)(4,1)S(1)} %copy-done.54, bf16[512,1024]{1,0:T(8,128)(2,1)S(1)} %pad_maximum_fusion.2), kind=kOutput, calls=%fused_computation.317 | convolution fusion | flops 85197312 | bytes 1673728 | tf_op jit(solution)/shard_map/sub | solution.py:92
  116.3 1.9 multiply_reduce_fusion
  119.1 1.1 fusion.59
  120.2 2.1 slice.375
  125.3 1.6 copy-done.3
  126.9 3.0 %fusion.17 = (f32[5120]{0:T(1024)S(1)}, f32[128]{0:T(128)S(1)}) fusion(bf16[128,5120]{0,1:T(8,128)(2,1)S(1)} %copy.70, f32[128,40,2,64]{0,3,2,1:T(8,128)S(1)} %pad_maximum_fusion, f32[128]{0:T(128)S(1)} %add_rsqrt_fusion.1, f32[5120]{0:T(1024)S(1)} %copy-done.44), kind=kLoop, calls=%fused_computation.25 | loop fusion | flops 4582272 | bytes 3974144 | tf_op jit(solution)/shard_map/reduce_sum | solution.py:78
  129.9 1.5 fusion.56
  131.4 1.5 fusion.55
  132.9 1.5 fusion.54
  134.5 1.5 fusion.53
  136.0 1.5 fusion.52
  137.5 1.5 fusion.51
  139.0 1.5 fusion.50
  140.5 2.1 slice.374
  142.6 1.2 collective-permute-start.6
  143.8 3.5 %fusion.13 = bf16[128,5120]{0,1:T(8,128)(2,1)S(1)} fusion(bf16[128,5120]{0,1:T(8,128)(2,1)S(1)} %copy.70, f32[128,40,2,64]{0,3,2,1:T(8,128)} %copy-done.3, f32[128]{0:T(128)S(1)} %broadcast_multiply_fusion.2, f32[5120]{0:T(1024)S(1)} %copy-done.44, f32[128]{0:T(128)S(1)} %add_rsqrt_fusion.1), kind=kLoop, calls=%fused_computation.21 | loop fusion | flops 5898240 | bytes 5264384 | tf_op jit(solution)/shard_map/convert_element_type | solution.py:173
  147.3 1.4 copy.131
  148.8 1.6 slice_add_fusion.1
  150.4 1.7 collective-permute-start.5
  152.1 3.1 %collective-permute-done.6 = bf16[256,1024]{0,1:T(8,128)(2,1)S(1)} collective-permute-done((bf16[256,1024]{0,1:T(8,128)(2,1)}, bf16[256,1024]{0,1:T(8,128)(2,1)S(1)}, u32[]{:S(2)}, u32[]{:S(2)}) %collective-permute-start.6) | collective-permute-done | bytes 524320 | tf_op jit(solution)/shard_map/ppermute | solution.py:29
  155.5 2.0 collective-permute-start.7
  160.6 11.0 %all-reduce.1 = (f32[5120]{0:T(1024)S(1)}, f32[1024]{0:T(1024)S(1)}) all-reduce(f32[5120]{0:T(1024)S(1)} %get-tuple-element.15, f32[1024]{0:T(1024)S(1)} %get-tuple-element.17), channel_id=1, replica_groups=mesh['groups'=2,'context_0'=4,'context_1'=16,'context_2'=2] {'context_0'}, use_global_device_ids=true, to_apply=%region_29.30 | all-reduce | flops 6144 | bytes 49152 | tf_op jit(solution)/shard_map/psum | solution.py:42
  171.6 45.1 %all-reduce = (f32[5120]{0:T(1024)S(1)}, f32[1024]{0:T(1024)S(1)}) all-reduce(f32[5120]{0:T(1024)S(1)} %get-tuple-element.21, f32[1024]{0:T(1024)S(1)} %get-tuple-element.22), channel_id=1, replica_groups=mesh['groups'=2,'context_0'=4,'context_1'=16,'context_2'=2] {'context_1'}, use_global_device_ids=true, to_apply=%region_30.31 | all-reduce | flops 6144 | bytes 49152 | tf_op jit(solution)/shard_map/psum | solution.py:42
  216.7 21.5 %all-reduce.2 = (f32[5120]{0:T(1024)}, f32[1024]{0:T(1024)}) all-reduce(f32[5120]{0:T(1024)S(1)} %get-tuple-element.19, f32[1024]{0:T(1024)S(1)} %get-tuple-element.20), channel_id=1, replica_groups=mesh['groups'=2,'context_0'=4,'context_1'=16,'context_2'=2] {'context_2'}, use_global_device_ids=true, to_apply=%region_31.32 | all-reduce | flops 6144 | bytes 49152 | tf_op jit(solution)/shard_map/psum | solution.py:42
  (197 shorter events, 26.2 us)
Async XLA Ops:
  0.6 5.7 %copy-start = (s32[16384]{0:T(1024)S(1)}, s32[16384]{0:T(1024)}, u32[]{:S(2)}) copy-start(s32[16384]{0:T(1024)} %param.14) | copy-start | bytes 196612
  0.6 0.7 copy-start.2
  1.4 6.1 %copy-start.43 = (bf16[128,1024]{1,0:T(8,128)(2,1)S(1)}, bf16[128,1024]{1,0:T(8,128)(2,1)}, u32[]{:S(2)}) copy-start(bf16[128,1024]{1,0:T(8,128)(2,1)} %param.9) | copy-start | bytes 786436
  4.9 3.8 %copy-start.55 = (f32[1024]{0:T(1024)S(1)}, f32[1024]{0:T(1024)}, u32[]{:S(2)}) copy-start(f32[1024]{0:T(1024)} %param.13) | copy-start | bytes 12292
  8.6 21.0 %copy-start.20 = (bf16[128,1024]{1,0:T(8,128)(2,1)S(1)}, bf16[128,1024]{1,0:T(8,128)(2,1)}, u32[]{:S(2)}) copy-start(bf16[128,1024]{1,0:T(8,128)(2,1)} %param.10) | copy-start | bytes 786436
  9.0 24.3 %copy-start.12 = (bf16[128,5120]{1,0:T(8,128)(2,1)S(1)}, bf16[128,5120]{1,0:T(8,128)(2,1)}, u32[]{:S(2)}) copy-start(bf16[128,5120]{1,0:T(8,128)(2,1)} %param.8) | copy-start | bytes 3932164
  9.1 31.4 %collective-permute-start = (bf16[128,1024]{1,0:T(8,128)(2,1)S(1)}, bf16[128,1024]{1,0:T(8,128)(2,1)}, u32[]{:S(2)}, u32[]{:S(2)}) collective-permute-start(bf16[128,1024]{1,0:T(8,128)(2,1)S(1)} %copy.74), channel_id=1, source_target_pairs={{0,1},{1,0},{2,3},{3,2},{4,5},{5,4},{6,7},{7,6},{8,9},{9,8},{10,11... | collective-permute-start | bytes 786440 | tf_op jit(solution)/shard_map/ppermute | solution.py:29
  29.7 17.9 %collective-permute-start.2 = (bf16[128,1024]{1,0:T(8,128)(2,1)S(1)}, bf16[128,1024]{1,0:T(8,128)(2,1)}, u32[]{:S(2)}, u32[]{:S(2)}) collective-permute-start(bf16[128,1024]{1,0:T(8,128)(2,1)S(1)} %copy-done.20), channel_id=1, source_target_pairs={{0,1},{1,0},{2,3},{3,2},{4,5},{5,4},{6,7},{7,6},{8,9},{9,8},{10,11... | collective-permute-start | bytes 786440 | tf_op jit(solution)/shard_map/ppermute | solution.py:29
  34.0 0.7 copy-start.44
  38.1 1.3 copy-start.13
  42.3 16.1 %collective-permute-start.1 = (bf16[256,1024]{1,0:T(8,128)(2,1)}, bf16[256,1024]{1,0:T(8,128)(2,1)}, u32[]{:S(2)}, u32[]{:S(2)}) collective-permute-start(bf16[256,1024]{1,0:T(8,128)(2,1)} %pad_maximum_fusion.3), channel_id=1, source_target_pairs={{0,2},{2,0},{1,3},{3,1},{4,6},{6,4},{5,7},{7,5},{8,10},{10,8},{9,1... | collective-permute-start | bytes 1572872 | tf_op jit(solution)/shard_map/ppermute | solution.py:29
  47.5 5.1 %copy-start.25 = (bf16[128,640]{1,0:T(8,128)(2,1)S(1)}, bf16[128,640]{1,0:T(8,128)(2,1)}, u32[]{:S(2)}) copy-start(bf16[128,640]{1,0:T(8,128)(2,1)} %get-tuple-element.45) | copy-start | bytes 491524
  47.5 5.9 %copy-start.24 = (bf16[128,640]{1,0:T(8,128)(2,1)S(1)}, bf16[128,640]{1,0:T(8,128)(2,1)}, u32[]{:S(2)}) copy-start(bf16[128,640]{1,0:T(8,128)(2,1)} %get-tuple-element.44) | copy-start | bytes 491524
  47.5 6.7 %copy-start.23 = (bf16[128,640]{1,0:T(8,128)(2,1)S(1)}, bf16[128,640]{1,0:T(8,128)(2,1)}, u32[]{:S(2)}) copy-start(bf16[128,640]{1,0:T(8,128)(2,1)} %get-tuple-element.43) | copy-start | bytes 491524
  47.5 7.5 %copy-start.22 = (bf16[128,640]{1,0:T(8,128)(2,1)S(1)}, bf16[128,640]{1,0:T(8,128)(2,1)}, u32[]{:S(2)}) copy-start(bf16[128,640]{1,0:T(8,128)(2,1)} %get-tuple-element.42) | copy-start | bytes 491524
  47.5 8.3 %copy-start.21 = (bf16[128,640]{1,0:T(8,128)(2,1)S(1)}, bf16[128,640]{1,0:T(8,128)(2,1)}, u32[]{:S(2)}) copy-start(bf16[128,640]{1,0:T(8,128)(2,1)} %get-tuple-element.41) | copy-start | bytes 491524
  49.4 17.8 %collective-permute-start.3 = (bf16[256,1024]{1,0:T(8,128)(2,1)}, bf16[256,1024]{1,0:T(8,128)(2,1)}, u32[]{:S(2)}, u32[]{:S(2)}) collective-permute-start(bf16[256,1024]{1,0:T(8,128)(2,1)} %pad_maximum_fusion.4), channel_id=1, source_target_pairs={{0,2},{2,0},{1,3},{3,1},{4,6},{6,4},{5,7},{7,5},{8,10},{10,8},{9,1... | collective-permute-start | bytes 1572872 | tf_op jit(solution)/shard_map/ppermute | solution.py:29
  56.7 2.9 %copy-start.41 = (bf16[128,640]{0,1:T(8,128)(2,1)S(1)}, bf16[128,640]{0,1:T(8,128)(2,1)}, u32[]{:S(2)}) copy-start(bf16[128,640]{0,1:T(8,128)(2,1)} %get-tuple-element.40) | copy-start | bytes 491524
  56.7 2.9 %copy-start.54 = (pred[128,512]{0,1:T(8,128)(4,1)S(1)}, pred[128,512]{0,1:T(8,128)(4,1)}, u32[]{:S(2)}) copy-start(pred[128,512]{0,1:T(8,128)(4,1)} %compare_and_fusion) | copy-start | bytes 196612
  59.6 9.5 %copy-start.53 = (bf16[128,640]{0,1:T(8,128)(2,1)S(1)}, bf16[128,640]{0,1:T(8,128)(2,1)}, u32[]{:S(2)}) copy-start(bf16[128,640]{0,1:T(8,128)(2,1)} %copy.190) | copy-start | bytes 491524
  69.0 1.8 copy-start.4
  72.4 2.5 %copy-start.38 = (bf16[128,640]{0,1:T(8,128)(2,1)S(1)}, bf16[128,640]{0,1:T(8,128)(2,1)}, u32[]{:S(2)}) copy-start(bf16[128,640]{0,1:T(8,128)(2,1)} %get-tuple-element.39) | copy-start | bytes 491524
  74.9 1.6 copy-start.46
  76.5 1.8 copy-start.6
  78.3 0.9 copy-start.39
  82.8 1.9 copy-start.7
  84.7 1.2 copy-start.36
  89.4 1.9 copy-start.8
  91.3 1.2 copy-start.34
  96.1 1.9 copy-start.9
  98.0 1.2 copy-start.32
  102.8 1.9 copy-start.10
  104.7 1.3 copy-start.30
  109.6 1.9 copy-start.11
  111.5 1.3 copy-start.28
  116.3 1.9 copy-start.5
  118.2 0.9 copy-start.26
  120.2 2.5 %copy-start.14 = (f32[128,5,128]{2,0,1:T(8,128)S(1)}, f32[128,5,128]{2,0,1:T(8,128)}, u32[]{:S(2)}) copy-start(f32[128,5,128]{2,0,1:T(8,128)} %convolution_multiply_fusion.13) | copy-start | bytes 983044
  120.2 2.6 %copy-start.15 = (f32[128,5,128]{2,0,1:T(8,128)S(1)}, f32[128,5,128]{2,0,1:T(8,128)}, u32[]{:S(2)}) copy-start(f32[128,5,128]{2,0,1:T(8,128)} %convolution_multiply_fusion.12) | copy-start | bytes 983044
  122.3 26.4 %collective-permute-start.4 = (bf16[256,1024]{0,1:T(8,128)(2,1)}, bf16[256,1024]{0,1:T(8,128)(2,1)}, u32[]{:S(2)}, u32[]{:S(2)}) collective-permute-start(bf16[256,1024]{0,1:T(8,128)(2,1)} %slice.375), channel_id=1, source_target_pairs={{0,2},{2,0},{1,3},{3,1},{4,6},{6,4},{5,7},{7,5},{8,10},{10,8},{9,1... | collective-permute-start | bytes 1572872 | tf_op jit(solution)/shard_map/ppermute | solution.py:29
  122.6 1.0 copy-start.16
  122.7 1.1 copy-start.17
  122.7 1.1 copy-start.18
  123.6 0.8 copy-start.42
  125.3 1.6 copy-start.3
  126.9 3.0 %copy-start.40 = (bf16[128,640]{0,1:T(8,128)(2,1)S(1)}, bf16[128,640]{0,1:T(8,128)(2,1)}, u32[]{:S(2)}) copy-start(bf16[128,640]{0,1:T(8,128)(2,1)} %get-tuple-element.39) | copy-start | bytes 491524
  126.9 3.0 %copy-start.47 = (bf16[128,640]{0,1:T(8,128)(2,1)S(1)}, bf16[128,640]{0,1:T(8,128)(2,1)}, u32[]{:S(2)}) copy-start(bf16[128,640]{0,1:T(8,128)(2,1)} %copy.191) | copy-start | bytes 491524
  129.9 1.5 copy-start.37
  129.9 1.5 copy-start.52
  131.4 1.5 copy-start.35
  131.4 1.5 copy-start.51
  132.9 1.5 copy-start.33
  132.9 1.5 copy-start.50
  134.5 1.5 copy-start.31
  134.5 1.5 copy-start.49
  136.0 1.5 copy-start.29
  136.0 1.5 copy-start.48
  137.5 1.5 copy-start.27
  137.5 1.5 copy-start.45
  142.6 12.7 %collective-permute-start.6 = (bf16[256,1024]{0,1:T(8,128)(2,1)}, bf16[256,1024]{0,1:T(8,128)(2,1)S(1)}, u32[]{:S(2)}, u32[]{:S(2)}) collective-permute-start(bf16[256,1024]{0,1:T(8,128)(2,1)} %slice.374), channel_id=1, source_target_pairs={{0,2},{2,0},{1,3},{3,1},{4,6},{6,4},{5,7},{7,5},{8,10},{10,8},{9,1... | collective-permute-start | bytes 1572872 | tf_op jit(solution)/shard_map/ppermute | solution.py:29
  148.8 6.5 %copy-start.19 = (f32[512,1024]{0,1:T(8,128)S(1)}, f32[512,1024]{0,1:T(8,128)}, u32[]{:S(2)}) copy-start(f32[512,1024]{0,1:T(8,128)} %fusion.50) | copy-start | bytes 6291460
  150.4 7.1 %collective-permute-start.5 = (bf16[128,1024]{0,1:T(8,128)(2,1)S(1)}, bf16[128,1024]{0,1:T(8,128)(2,1)S(1)}, u32[]{:S(2)}, u32[]{:S(2)}) collective-permute-start(bf16[128,1024]{0,1:T(8,128)(2,1)S(1)} %slice.377), channel_id=1, source_target_pairs={{0,1},{1,0},{2,3},{3,2},{4,5},{5,4},{6,7},{7,6},{8,9},{9,8},{10,11... | collective-permute-start | bytes 786440 | tf_op jit(solution)/shard_map/ppermute | solution.py:29
  155.5 3.2 %collective-permute-start.7 = (bf16[128,1024]{0,1:T(8,128)(2,1)S(1)}, bf16[128,1024]{0,1:T(8,128)(2,1)S(1)}, u32[]{:S(2)}, u32[]{:S(2)}) collective-permute-start(bf16[128,1024]{0,1:T(8,128)(2,1)S(1)} %slice.376), channel_id=1, source_target_pairs={{0,1},{1,0},{2,3},{3,2},{4,5},{5,4},{6,7},{7,6},{8,9},{9,8},{10,11... | collective-permute-start | bytes 786440 | tf_op jit(solution)/shard_map/ppermute | solution.py:29
  158.7 79.5 %copy-start.1 = (s32[16384]{0:T(1024)S(1)}, s32[16384]{0:T(1024)}, u32[]{:S(2)}) copy-start(s32[16384]{0:T(1024)} %param.14) | copy-start | bytes 196612
where the time goes:
time: 239 us; the launch traced here: 238 us
  blocking collectives  77.5 us (32%)
  matrix products  60.7 us (25%)
  local copies, waits for them, and re-layouts  39.1 us (16%)
  starting transfers between devices  27.5 us (12%)
  other arithmetic  22.1 us (9%)
  waiting for transfers between devices  9.75 us (4%)
    psum x3, blocking collectives, by_axis(): array = lax.psum(array, axis)  77.5 us
    ppermute x8, starting transfers between devices, swapped(): return lax.ppermute(block, axis, route)  27.5 us
    unnamed x134, local copies, waits for them, and re-layouts  21.6 us
    sub x8, matrix products, head_gradients(): expo = jnp.exp(scores - row_max)  18.1 us
    dot_general x8, matrix products, head_gradients(): jnp.einsum('qgd,kd->gqk', grad_heads, value_rows, preferred_element_type=...  15 us
    dot_general x8, matrix products, head_gradients(): jnp.einsum('gqk,qgd->kd', probs_low, grad_heads, preferred_element_type=j...  13 us
    ppermute x8, waiting for transfers between devices, swapped(): return lax.ppermute(block, axis, route)  9.75 us
    dot_general x8, matrix products, head_gradients(): jnp.einsum('gqk,qgd->kd', dscores, query_heads, preferred_element_type=jn...  8.41 us
  transfers between devices with their start and end apart: 8, of which 3 were waited for; matrix products, arithmetic and copies ran while one was open for 22% of the time, Pallas kernels for 0%

commit v1 on v0

v1 whole, which is shorter than its diff:
```python
import functools
import math

import jax
import jax.numpy as jnp
import numpy as np
from jax import lax
from jax.experimental import pallas as pl
from jax.experimental.pallas import tpu as pltpu
from jax.sharding import Mesh
from jax.sharding import PartitionSpec as P

QUERY_HEADS = 40
KEY_VALUE_HEADS = 8
HEADS_PER = QUERY_HEADS // KEY_VALUE_HEADS
HEAD_SIZE = 128
SPAN = 64
LENGTH = 512
SPANS = LENGTH // SPAN
TOK = 128
QROWS = HEADS_PER * TOK
CONTEXT = ("context_0", "context_1", "context_2")
GROUPS_CONTEXT = ("groups", "context_0", "context_1", "context_2")
NORM_EPS = 1e-06
ROPE_BASE = 500000.0
SCALE = HEAD_SIZE ** (-0.5)
SCALE2 = SCALE * math.log2(math.e)
MESH = pl.DeviceIdType.MESH
F32 = jnp.float32
BF16 = jnp.bfloat16


def rope_tables():
    half = HEAD_SIZE // 2
    inv_freq = np.power(ROPE_BASE, -2.0 * np.arange(half) / HEAD_SIZE)
    angles = np.arange(LENGTH)[:, None] * inv_freq[None, :]
    cosine, sine = np.cos(angles), np.sin(angles)
    return (
        np.concatenate([cosine, cosine], axis=1).astype(np.float32),
        np.concatenate([-sine, sine], axis=1).astype(np.float32),
    )


def swap_halves(x):
    return pltpu.roll(x, HEAD_SIZE // 2, 1)


def kernel(
    nx, nz, nc,
    q_hbm, k_hbm, v_hbm, g_hbm, qg_ref, kg_ref, seg_ref, cos_ref, sin_ref, lay_ref,
    qgrad_hbm, kgrad_hbm, vgrad_hbm, qgain_ref, kgain_ref,
    q_vm, g_vm, k_vm, kv, qr, st, dp, pt, ds, dqw, dkw,
    bias, segcol, cosk, sink, rqb, rkb, inner,
    own, mid, sd, rd, si, ri, outb,
    gpart, rs, zb, ag,
    in_sem, kin_sem, vin_sem,
    z_send, z_recv, c_send, c_recv, f_send, f_recv,
    d_send, d_recv, i_send, i_recv,
    rs_send, rs_recv, zb_send, zb_recv, ag_send, ag_recv, out_sem,
):
    xi = lax.axis_index("context_0")
    zi = lax.axis_index("context_1")
    ci = lax.axis_index("context_2")
    rank = xi * nc + ci
    seq = xi * (nz // 2) + zi // 2
    z_flip = zi + 1 - 2 * lax.rem(zi, 2)
    partner = {"context_2": 1 - ci}
    across = {"context_1": z_flip}

    def rank_peer(other):
        return {"context_0": other // nc, "context_2": lax.rem(other, nc)}

    def k_in(h):
        cols = pl.ds(pl.multiple_of(h * HEAD_SIZE, HEAD_SIZE), HEAD_SIZE)
        return pltpu.make_async_copy(k_hbm.at[:, cols], k_vm.at[h], kin_sem.at[h])

    def v_in(h):
        cols = pl.ds(pl.multiple_of(h * HEAD_SIZE, HEAD_SIZE), HEAD_SIZE)
        return pltpu.make_async_copy(v_hbm.at[:, cols], kv.at[h, 1, 0:TOK], vin_sem.at[h])

    def q_in(h, j):
        cols = pl.ds(pl.multiple_of((h * HEADS_PER + j) * HEAD_SIZE, HEAD_SIZE), HEAD_SIZE)
        rows = pl.ds(j * TOK, TOK)
        return pltpu.make_async_copy(q_hbm.at[:, cols], q_vm.at[h, rows], in_sem.at[0, h, j])

    def g_in(h, j):
        cols = pl.ds(pl.multiple_of((h * HEADS_PER + j) * HEAD_SIZE, HEAD_SIZE), HEAD_SIZE)
        rows = pl.ds(j * TOK, TOK)
        return pltpu.make_async_copy(g_hbm.at[:, cols], g_vm.at[h, rows], in_sem.at[1, h, j])

    @pl.loop(0, KEY_VALUE_HEADS)
    def _(h):
        k_in(h).start()
        v_in(h).start()

    @pl.loop(0, KEY_VALUE_HEADS)
    def _(h):
        for j in range(HEADS_PER):
            q_in(h, j).start()
            g_in(h, j).start()

    barrier = pltpu.get_barrier_semaphore()
    for d in range(1, nx * nc):
        pl.semaphore_signal(
            barrier, inc=1, device_id=rank_peer(jnp.bitwise_xor(rank, d)), device_id_type=MESH
        )
    for d in range(1, nz):
        pl.semaphore_signal(
            barrier, inc=1, device_id={"context_1": lax.rem(zi + d, nz)}, device_id_type=MESH
        )

    my_local = 2 * lax.rem(zi, 2) + ci
    sub_iota = lax.broadcasted_iota(jnp.int32, (SPAN, TOK), 0)
    lane = lax.broadcasted_iota(jnp.int32, (8, TOK), 1)
    spans = []
    for flip in (0, 2, 1, 3):
        holder = jnp.bitwise_xor(my_local, flip)
        for part in range(2):
            slot = lay_ref[seq * SPANS + 2 * holder + part]
            spans.append(jnp.bitwise_and(jnp.full((8, TOK), slot, jnp.int32), SPANS - 1))

    def pick(span, table):
        chosen = table[0:SPAN, :]
        wide = jnp.concatenate([span] * (SPAN // 8), axis=0)
        for at in range(1, SPANS):
            chosen = jnp.where(wide == at, table[at * SPAN : (at + 1) * SPAN, :], chosen)
        return chosen

    for index, span in enumerate(spans):
        rows = slice(index * SPAN, (index + 1) * SPAN)
        cosk[rows, :] = pick(span, cos_ref)
        sink[rows, :] = pick(span, sin_ref)

    @pl.loop(0, KEY_VALUE_HEADS)
    def _(h):
        k_in(h).wait()

    acc = jnp.zeros((TOK, HEAD_SIZE), F32)
    for h in range(KEY_VALUE_HEADS):
        x = k_vm[h].astype(F32)
        acc = acc + x * x
    mean_sq = jnp.sum(acc, axis=1, keepdims=True) * (1.0 / (KEY_VALUE_HEADS * HEAD_SIZE))
    rkb[...] = jnp.broadcast_to(lax.rsqrt(mean_sq + NORM_EPS), (TOK, HEAD_SIZE))

    @pl.loop(0, KEY_VALUE_HEADS)
    def _(h):
        x = k_vm[h].astype(F32)
        normed = x * rkb[...] * kg_ref[pl.ds(h, 1), :]
        kv[h, 0, 0:TOK] = (normed * cosk[0:TOK] + swap_halves(normed) * sink[0:TOK]).astype(BF16)
        v_in(h).wait()

    pl.semaphore_wait(barrier, nx * nc - 1 + nz - 1)

    def to_across(h):
        return pltpu.make_async_remote_copy(
            kv.at[h, :, 0:TOK], kv.at[h, :, TOK : 2 * TOK], z_send.at[h], z_recv.at[h],
            device_id=across, device_id_type=MESH,
        )

    def to_partner(h):
        return pltpu.make_async_remote_copy(
            kv.at[h, :, 0:TOK], kv.at[h, :, 2 * TOK : 3 * TOK], c_send.at[h], c_recv.at[h],
            device_id=partner, device_id_type=MESH,
        )

    def forward(h):
        return pltpu.make_async_remote_copy(
            kv.at[h, :, TOK : 2 * TOK], kv.at[h, :, 3 * TOK : 4 * TOK], f_send.at[h], f_recv.at[h],
            device_id=partner, device_id_type=MESH,
        )

    def grads_to_partner(h):
        return pltpu.make_async_remote_copy(
            sd.at[h], rd.at[h], d_send.at[h], d_recv.at[h],
            device_id=partner, device_id_type=MESH,
        )

    def grads_across(h):
        return pltpu.make_async_remote_copy(
            si.at[h], ri.at[h], i_send.at[h], i_recv.at[h],
            device_id=across, device_id_type=MESH,
        )

    @pl.loop(0, KEY_VALUE_HEADS)
    def _(h):
        to_across(h).start()
        to_partner(h).start()

    first = lane < SPAN
    query_span = jnp.where(first, spans[0], spans[1])
    doc_row = jnp.zeros((8, TOK), F32)
    for part in range(LENGTH // TOK):
        row = seg_ref[pl.ds(seq * (LENGTH // TOK) + part, 1), :].astype(F32)
        segcol[part * TOK : (part + 1) * TOK, :] = jnp.transpose(
            jnp.broadcast_to(row, (TOK, TOK))
        )
        row = jnp.broadcast_to(row, (8, TOK))
        turned = pltpu.roll(row, SPAN, 1)
        doc_row = jnp.where(query_span == 2 * part, jnp.where(first, row, turned), doc_row)
        doc_row = jnp.where(query_span == 2 * part + 1, jnp.where(first, turned, row), doc_row)
    doc_row = doc_row[0:1, :]
    pos_row = (query_span * SPAN + jnp.bitwise_and(lane, SPAN - 1))[0:1, :]
    for index, span in enumerate(spans):
        doc_col = pick(span, segcol)
        pos_col = span[0:1, :] * SPAN + sub_iota
        allowed = (doc_col == doc_row) & (pos_col <= pos_row)
        bias[index * SPAN : (index + 1) * SPAN, :] = jnp.where(allowed, 0.0, -jnp.inf)

    @pl.loop(0, KEY_VALUE_HEADS)
    def _(h):
        for j in range(HEADS_PER):
            q_in(h, j).wait()
            g_in(h, j).wait()

    inner[...] = jnp.zeros((TOK, HEAD_SIZE), F32)

    @pl.loop(0, KEY_VALUE_HEADS)
    def _(h):
        total = inner[...]
        for j in range(HEADS_PER):
            x = q_vm[h, j * TOK : (j + 1) * TOK].astype(F32)
            total = total + x * x
        inner[...] = total

    mean_sq = jnp.sum(inner[...], axis=1, keepdims=True) * (1.0 / (QUERY_HEADS * HEAD_SIZE))
    rqb[...] = jnp.broadcast_to(lax.rsqrt(mean_sq + NORM_EPS), (TOK, HEAD_SIZE))
    inner[...] = jnp.zeros((TOK, HEAD_SIZE), F32)

    z_take = to_across(0)
    z_take.wait_recv()
    forward(0).start()

    def add_and_send(h):
        grads_to_partner(h).wait_recv()
        for s in range(2):
            si[h, s] = (mid[h, s] + rd[h, s, TOK : 2 * TOK]).astype(BF16)
        grads_across(h).start()

    CH = 64

    @pl.loop(0, KEY_VALUE_HEADS)
    def _(h):
        @pl.when(h < KEY_VALUE_HEADS - 1)
        def _():
            to_across(h + 1).wait_recv()
            forward(h + 1).start()

        for j in range(HEADS_PER):
            x = q_vm[h, j * TOK : (j + 1) * TOK].astype(F32)
            normed = x * rqb[...] * qg_ref[pl.ds(h * HEADS_PER + j, 1), :]
            qr[j * TOK : (j + 1) * TOK] = (
                normed * cosk[0:TOK] + swap_halves(normed) * sink[0:TOK]
            ).astype(BF16)

        to_partner(h).wait_recv()
        forward(h).wait_recv()
        nt = (((1,), (1,)), ((), ()))
        st[...] = lax.dot_general(kv[h, 0], qr[...], nt, preferred_element_type=F32)
        dp[...] = lax.dot_general(kv[h, 1], g_vm[h], nt, preferred_element_type=F32)

        for j in range(HEADS_PER):
            cols = slice(j * TOK, (j + 1) * TOK)
            top = jnp.full((8, TOK), -jnp.inf, F32)
            for c in range(LENGTH // CH):
                rows = slice(c * CH, (c + 1) * CH)
                s = st[rows, cols] * SCALE2 + bias[rows, :]
                st[rows, cols] = s
                top = jnp.maximum(top, jnp.max(s.reshape(CH // 8, 8, TOK), axis=0))
            top = jnp.max(top, axis=0, keepdims=True)
            weight = jnp.zeros((8, TOK), F32)
            delta = jnp.zeros((8, TOK), F32)
            for c in range(LENGTH // CH):
                rows = slice(c * CH, (c + 1) * CH)
                p = jnp.exp2(st[rows, cols] - top)
                st[rows, cols] = p
                weight = weight + jnp.sum(p.reshape(CH // 8, 8, TOK), axis=0)
                delta = delta + jnp.sum((p * dp[rows, cols]).reshape(CH // 8, 8, TOK), axis=0)
            norm = 1.0 / jnp.sum(weight, axis=0, keepdims=True)
            delta = jnp.sum(delta, axis=0, keepdims=True) * norm
            for c in range(LENGTH // CH):
                rows = slice(c * CH, (c + 1) * CH)
                p = st[rows, cols] * norm
                pt[rows, cols] = p.astype(BF16)
                ds[rows, cols] = (p * (dp[rows, cols] - delta)).astype(BF16)

        tn = (((0,), (0,)), ((), ()))
        dq = lax.dot_general(ds[...], kv[h, 0], tn, preferred_element_type=F32)
        for j in range(HEADS_PER):
            part = dq[j * TOK : (j + 1) * TOK] * SCALE
            part = part * cosk[0:TOK] - swap_halves(part) * sink[0:TOK]
            x = q_vm[h, j * TOK : (j + 1) * TOK].astype(F32)
            gpart[h, j : j + 1, :] = jnp.sum(part * x * rqb[...], axis=0, keepdims=True)
            weighted = part * qg_ref[pl.ds(h * HEADS_PER + j, 1), :]
            dqw[h, j * TOK : (j + 1) * TOK] = weighted
            inner[...] = inner[...] + weighted * x

        nn = (((1,), (0,)), ((), ()))
        dv = lax.dot_general(pt[...], g_vm[h], nn, preferred_element_type=F32)
        own[h, 1] = dv[0:TOK]
        mid[h, 1] = dv[TOK : 2 * TOK]
        sd[h, 1] = dv[2 * TOK :]
        dk = lax.dot_general(ds[...], qr[...], nn, preferred_element_type=F32) * SCALE
        own[h, 0] = dk[0:TOK]
        mid[h, 0] = dk[TOK : 2 * TOK]
        sd[h, 0] = dk[2 * TOK :]
        grads_to_partner(h).start()

        total = jnp.zeros((8, HEAD_SIZE), F32)
        for c in range(4):
            rows = slice(c * TOK, (c + 1) * TOK)
            d_part = dk[rows]
            k_part = kv[h, 0, rows].astype(F32)
            d_part = d_part * cosk[rows] - swap_halves(d_part) * sink[rows]
            k_part = k_part * cosk[rows] - swap_halves(k_part) * sink[rows]
            total = total + jnp.sum((d_part * k_part).reshape(TOK // 8, 8, HEAD_SIZE), axis=0)
        gpart[h, HEADS_PER : HEADS_PER + 1, :] = (
            jnp.sum(total, axis=0, keepdims=True) / kg_ref[pl.ds(h, 1), :]
        )
        gpart[h, HEADS_PER + 1 :, :] = jnp.zeros((7 - HEADS_PER, HEAD_SIZE), F32)

        @pl.when(h > 0)
        def _():
            add_and_send(h - 1)

    def shard_out(d):
        other = jnp.bitwise_xor(rank, d)
        return pltpu.make_async_remote_copy(
            gpart.at[other], rs.at[d], rs_send.at[d], rs_recv.at[d],
            device_id=rank_peer(other), device_id_type=MESH,
        )

    def z_out(d):
        return pltpu.make_async_remote_copy(
            zb.at[zi], zb.at[zi], zb_send.at[d], zb_recv.at[zi],
            device_id={"context_1": lax.rem(zi + d, nz)}, device_id_type=MESH,
        )

    def z_got(d):
        source = lax.rem(zi + d, nz)
        return pltpu.make_async_remote_copy(
            zb.at[source], zb.at[source], zb_send.at[d], zb_recv.at[source],
            device_id={"context_1": source}, device_id_type=MESH,
        )

    def total_out(d):
        other = jnp.bitwise_xor(rank, d)
        return pltpu.make_async_remote_copy(
            ag.at[rank], ag.at[rank], ag_send.at[d], ag_recv.at[rank],
            device_id=rank_peer(other), device_id_type=MESH,
        )

    def total_got(d):
        other = jnp.bitwise_xor(rank, d)
        return pltpu.make_async_remote_copy(
            ag.at[other], ag.at[other], ag_send.at[d], ag_recv.at[other],
            device_id=rank_peer(other), device_id_type=MESH,
        )

    for d in range(1, nx * nc):
        shard_out(d).start()

    add_and_send(KEY_VALUE_HEADS - 1)

    summed = gpart[rank]
    for d in range(1, nx * nc):
        shard_out(d).wait_recv()
        summed = summed + rs[d]
    zb[zi] = summed
    for d in range(1, nz):
        z_out(d).start()

    inner_q = jnp.sum(inner[...], axis=1, keepdims=True) * (1.0 / (QUERY_HEADS * HEAD_SIZE))
    cube = rqb[...] * rqb[...] * rqb[...] * inner_q
    inner[...] = cube

    def q_out(h, j):
        cols = pl.ds(pl.multiple_of((h * HEADS_PER + j) * HEAD_SIZE, HEAD_SIZE), HEAD_SIZE)
        rows = pl.ds(j * TOK, TOK)
        return pltpu.make_async_copy(outb.at[h, rows], qgrad_hbm.at[:, cols], out_sem.at[h, j])

    @pl.loop(0, KEY_VALUE_HEADS)
    def _(h):
        for j in range(HEADS_PER):
            rows = slice(j * TOK, (j + 1) * TOK)
            x = q_vm[h, rows].astype(F32)
            outb[h, rows] = (rqb[...] * dqw[h, rows] - x * inner[...]).astype(BF16)
            q_out(h, j).start()

    for d in range(1, nz):
        z_got(d).wait_recv()
    total = zb[0]
    for d in range(1, nz):
        total = total + zb[d]
    ag[rank] = total
    for d in range(1, nx * nc):
        total_out(d).start()

    def k_out(h, s, out):
        cols = pl.ds(pl.multiple_of(h * HEAD_SIZE, HEAD_SIZE), HEAD_SIZE)
        return pltpu.make_async_copy(si.at[h, s], out.at[:, cols], out_sem.at[h, HEADS_PER + s])

    inner[...] = jnp.zeros((TOK, HEAD_SIZE), F32)

    @pl.loop(0, KEY_VALUE_HEADS)
    def _(h):
        grads_across(h).wait()
        d_part = own[h, 0] + rd[h, 0, 0:TOK] + ri[h, 0].astype(F32)
        d_part = d_part * cosk[0:TOK] - swap_halves(d_part) * sink[0:TOK]
        weighted = d_part * kg_ref[pl.ds(h, 1), :]
        dkw[h] = weighted
        inner[...] = inner[...] + weighted * k_vm[h].astype(F32)
        si[h, 1] = (own[h, 1] + rd[h, 1, 0:TOK] + ri[h, 1].astype(F32)).astype(BF16)
        k_out(h, 1, vgrad_hbm).start()

    inner_k = jnp.sum(inner[...], axis=1, keepdims=True) * (1.0 / (KEY_VALUE_HEADS * HEAD_SIZE))
    inner[...] = rkb[...] * rkb[...] * rkb[...] * inner_k

    @pl.loop(0, KEY_VALUE_HEADS)
    def _(h):
        si[h, 0] = (rkb[...] * dkw[h] - k_vm[h].astype(F32) * inner[...]).astype(BF16)
        k_out(h, 0, kgrad_hbm).start()

    for d in range(1, nx * nc):
        total_got(d).wait_recv()
    for h in range(KEY_VALUE_HEADS):
        qgain_ref[h * HEADS_PER : (h + 1) * HEADS_PER, :] = ag[h, 0:HEADS_PER, :]
        kgain_ref[h : h + 1, :] = ag[h, HEADS_PER : HEADS_PER + 1, :]

    @pl.loop(0, KEY_VALUE_HEADS)
    def _(h):
        to_across(h).wait_send()
        to_partner(h).wait_send()
        forward(h).wait_send()
        grads_to_partner(h).wait_send()
        for j in range(HEADS_PER):
            q_out(h, j).wait()
        k_out(h, 0, kgrad_hbm).wait()
        k_out(h, 1, vgrad_hbm).wait()

    for d in range(1, nx * nc):
        shard_out(d).wait_send()
        total_out(d).wait_send()
    for d in range(1, nz):
        z_out(d).wait_send()


def body(nx, nz, nc, query_proj, key_proj, values, grad_out, query_gain, key_gain, segments, layout):
    cos_table, sin_table = rope_tables()
    assert nx * nc == KEY_VALUE_HEADS or nx * nc < KEY_VALUE_HEADS
    kvh, hs = KEY_VALUE_HEADS, HEAD_SIZE
    any_spec = pl.BlockSpec(memory_space=pl.ANY)
    vm_spec = pl.BlockSpec(memory_space=pltpu.VMEM)
    dma = pltpu.SemaphoreType.DMA
    out = pl.pallas_call(
        functools.partial(kernel, nx, nz, nc),
        out_shape=(
            jax.ShapeDtypeStruct(query_proj.shape, BF16),
            jax.ShapeDtypeStruct(key_proj.shape, BF16),
            jax.ShapeDtypeStruct(values.shape, BF16),
            jax.ShapeDtypeStruct((QUERY_HEADS, hs), F32),
            jax.ShapeDtypeStruct((kvh, hs), F32),
        ),
        in_specs=[any_spec] * 4 + [vm_spec] * 5 + [pl.BlockSpec(memory_space=pltpu.SMEM)],
        out_specs=(any_spec, any_spec, any_spec, vm_spec, vm_spec),
        scratch_shapes=[
            pltpu.VMEM((kvh, QROWS, hs), BF16),
            pltpu.VMEM((kvh, QROWS, hs), BF16),
            pltpu.VMEM((kvh, TOK, hs), BF16),
            pltpu.VMEM((kvh, 2, LENGTH, hs), BF16),
            pltpu.VMEM((QROWS, hs), BF16),
            pltpu.VMEM((LENGTH, QROWS), F32),
            pltpu.VMEM((LENGTH, QROWS), F32),
            pltpu.VMEM((LENGTH, QROWS), BF16),
            pltpu.VMEM((LENGTH, QROWS), BF16),
            pltpu.VMEM((kvh, QROWS, hs), F32),
            pltpu.VMEM((kvh, TOK, hs), F32),
            pltpu.VMEM((LENGTH, TOK), F32),
            pltpu.VMEM((LENGTH, TOK), F32),
            pltpu.VMEM((LENGTH, hs), F32),
            pltpu.VMEM((LENGTH, hs), F32),
            pltpu.VMEM((TOK, hs), F32),
            pltpu.VMEM((TOK, hs), F32),
            pltpu.VMEM((TOK, hs), F32),
            pltpu.VMEM((kvh, 2, TOK, hs), F32),
            pltpu.VMEM((kvh, 2, TOK, hs), F32),
            pltpu.VMEM((kvh, 2, 2 * TOK, hs), F32),
            pltpu.VMEM((kvh, 2, 2 * TOK, hs), F32),
            pltpu.VMEM((kvh, 2, TOK, hs), BF16),
            pltpu.VMEM((kvh, 2, TOK, hs), BF16),
            pltpu.VMEM((kvh, QROWS, hs), BF16),
            pltpu.VMEM((kvh, 8, hs), F32),
            pltpu.VMEM((nx * nc, 8, hs), F32),
            pltpu.VMEM((nz, 8, hs), F32),
            pltpu.VMEM((kvh, 8, hs), F32),
            dma((2, kvh, HEADS_PER)), dma((kvh,)), dma((kvh,)),
            dma((kvh,)), dma((kvh,)), dma((kvh,)), dma((kvh,)), dma((kvh,)), dma((kvh,)),
            dma((kvh,)), dma((kvh,)), dma((kvh,)), dma((kvh,)),
            dma((nx * nc,)), dma((nx * nc,)), dma((nz,)), dma((nz,)), dma((kvh,)), dma((kvh,)),
            dma((kvh, HEADS_PER + 2)),
        ],
        compiler_params=pltpu.CompilerParams(
            collective_id=0, has_side_effects=True, vmem_limit_bytes=56 * 1024 * 1024
        ),
    )(
        query_proj, key_proj, values, grad_out,
        query_gain.reshape(QUERY_HEADS, hs), key_gain.reshape(kvh, hs),
        segments.reshape(-1, TOK), jnp.asarray(cos_table), jnp.asarray(sin_table), layout,
    )
    return out[0], out[1], out[2], out[3].reshape(-1), out[4].reshape(-1)


def solution(mesh):
    nx, nz, nc = 4, 16, 2
    split = Mesh(mesh.devices.reshape(mesh.shape["groups"], nx, nz, nc), GROUPS_CONTEXT)
    tokens = P(GROUPS_CONTEXT, None)
    return jax.shard_map(
        functools.partial(body, nx, nz, nc),
        mesh=split,
        in_specs=(tokens, tokens, tokens, tokens, P(), P(), P("groups"), P("groups")),
        out_specs=(tokens, tokens, tokens, P("groups"), P("groups")),
        check_vma=False,
    )
```

time: 239 us -> 75.1 us (0.31)
  blocking collectives: 77.5 us -> 0 us
  Pallas kernels: 0 us -> 69.1 us
  matrix products: 60.7 us -> 0 us
  local copies, waits for them, and re-layouts: 39.1 us -> 5.13 us
  starting transfers between devices: 27.5 us -> 0 us
  other arithmetic: 22.1 us -> 0 us
  waiting for transfers between devices: 9.75 us -> 0 us
    psum x3 -> x0, blocking collectives: 77.5 us -> none  [by_axis(): array = lax.psum(array, axis)]
    pallas_call x0 -> x1, Pallas kernels: none -> 69.1 us  [body(): pl.pallas_call(functools.partial(kernel, nx, nz, nc), out_shape=(jax.Shap...]
    dot_general x32 -> x0, matrix products: 42.6 us -> none  [the longest x8 15 us: head_gradients(): jnp.einsum('qgd,kd->gqk', grad_heads, value_rows, preferred_element_type=...]
    ppermute x8 -> x0, starting transfers between devices: 27.5 us -> none  [swapped(): return lax.ppermute(block, axis, route)]
    sub x8 -> x0, matrix products: 18.1 us -> none  [head_gradients(): expo = jnp.exp(scores - row_max)]
    unnamed x134 -> x13, local copies, waits for them, and re-layouts: 21.6 us -> 5.13 us
    ppermute x8 -> x0, waiting for transfers between devices: 9.75 us -> none  [swapped(): return lax.ppermute(block, axis, route)]
    gather x4 -> x0, local copies, waits for them, and re-layouts: 9.04 us -> none  [the longest x2 4.76 us: token_info(): positions = jnp.take(layout, slot_ids) * SPAN + local_index[None, :] % SPAN]
  transfers between devices with their start and end apart: 8 -> 0, of which waited for: 3 -> 0; matrix products, arithmetic and copies ran while one was open for 22% -> 0% of each run, Pallas kernels for 0% -> 0%
where the time goes in v1:
time: 75.1 us; the launch traced here: 74.9 us
  Pallas kernels  69.1 us (92%)
  local copies, waits for them, and re-layouts  5.13 us (7%)
    pallas_call x1, Pallas kernels, body(): pl.pallas_call(functools.partial(kernel, nx, nz, nc), out_shape=(jax.Shap...  69.1 us
    unnamed x13, local copies, waits for them, and re-layouts  5.13 us

profile of v1, /device:TPU:33, one launch (start us, length us, event | category | flops | bytes accessed | tf_op | source)
XLA Modules:
  0.0 74.9 jit_solution(8089301877759225441)
XLA Ops:
  0.6 69.1 %shard_map.137 = (bf16[128,5120]{1,0:T(8,128)(2,1)}, bf16[128,1024]{1,0:T(8,128)(2,1)}, bf16[128,1024]{1,0:T(8,128)(2,1)}, f32[40,128]{1,0:T(8,128)}, f32[8,128]{1,0:T(8,128)}) custom-call(bf16[128,5120]{1,0:T(8,128)(2,1)} %q_hbm.1, bf16[128,1024]{1,0:T(8,128)(2,1)} %k_hbm.1, bf16[128,1024]{1,0:T(8,128)(2,1)} %v_hbm.1, bf16[128,5120]{1,0:T(8,128)(2,1)} %g_hbm.1, ...), custom_call_target="tpu_custom_call" | custom-call | tf_op jit(solution)/shard_map/pallas_call | solution.py:454
  69.7 0.0 copy-start.1
  69.7 0.0 copy-start
  69.7 0.0 copy-start.2
  69.8 0.0 copy-start.3
  69.8 2.5 %copy.20 = bf16[128,5120]{1,0:T(8,128)(2,1)} copy(bf16[128,5120]{1,0:T(8,128)(2,1)} %get-tuple-element.20) | data formatting | bytes 2621440
  72.3 0.0 copy-done.1
  72.3 0.7 copy.21
  73.0 0.0 copy-done
  73.0 0.7 copy.22
  73.7 0.0 copy-done.2
  73.7 0.6 copy.23
  74.3 0.0 copy-done.3
  74.3 0.6 copy.24
Async XLA Ops:
  69.7 2.6 %copy-start.1 = (bf16[128,1024]{1,0:T(8,128)(2,1)S(1)}, bf16[128,1024]{1,0:T(8,128)(2,1)}, u32[]{:S(2)}) copy-start(bf16[128,1024]{1,0:T(8,128)(2,1)} %get-tuple-element.21) | copy-start | bytes 786436
  69.7 3.2 %copy-start = (bf16[128,1024]{1,0:T(8,128)(2,1)S(1)}, bf16[128,1024]{1,0:T(8,128)(2,1)}, u32[]{:S(2)}) copy-start(bf16[128,1024]{1,0:T(8,128)(2,1)} %get-tuple-element.22) | copy-start | bytes 786436
  69.7 3.9 %copy-start.2 = (f32[40,128]{1,0:T(8,128)S(1)}, f32[40,128]{1,0:T(8,128)}, u32[]{:S(2)}) copy-start(f32[40,128]{1,0:T(8,128)} %get-tuple-element.13) | copy-start | bytes 61444
  69.8 4.5 %copy-start.3 = (f32[8,128]{1,0:T(8,128)S(1)}, f32[8,128]{1,0:T(8,128)}, u32[]{:S(2)}) copy-start(f32[8,128]{1,0:T(8,128)} %get-tuple-element.14) | copy-start | bytes 12292

commit v2 on v1

--- a/solution.py
+++ b/solution.py
@@ -47,13 +47,14 @@
 
 def kernel(
     nx, nz, nc,
-    q_hbm, k_hbm, v_hbm, g_hbm, qg_ref, kg_ref, seg_ref, cos_ref, sin_ref, lay_ref,
+    q_hbm, k_hbm, v_hbm, g_hbm, cos_hbm, sin_hbm, seg_hbm, qg_ref, kg_ref, lay_ref,
     qgrad_hbm, kgrad_hbm, vgrad_hbm, qgain_ref, kgain_ref,
+    cos_ref, sin_ref, seg_ref,
     q_vm, g_vm, k_vm, kv, qr, st, dp, pt, ds, dqw, dkw,
-    bias, segcol, cosk, sink, rqb, rkb, inner,
+    bias, segcol, cosk, sink, cq, sq, rqb, rkb, inner,
     own, mid, sd, rd, si, ri, outb,
     gpart, rs, zb, ag,
-    in_sem, kin_sem, vin_sem,
+    in_sem, kin_sem, vin_sem, tab_sem,
     z_send, z_recv, c_send, c_recv, f_send, f_recv,
     d_send, d_recv, i_send, i_recv,
     rs_send, rs_recv, zb_send, zb_recv, ag_send, ag_recv, out_sem,
@@ -88,16 +89,17 @@
         rows = pl.ds(j * TOK, TOK)
         return pltpu.make_async_copy(g_hbm.at[:, cols], g_vm.at[h, rows], in_sem.at[1, h, j])
 
-    @pl.loop(0, KEY_VALUE_HEADS)
-    def _(h):
+    tables = [
+        pltpu.make_async_copy(source, target, tab_sem.at[index])
+        for index, (source, target) in enumerate(
+            ((cos_hbm, cos_ref), (sin_hbm, sin_ref), (seg_hbm, seg_ref))
+        )
+    ]
+    for h in range(KEY_VALUE_HEADS):
+        v_in(h).start()
         k_in(h).start()
-        v_in(h).start()
-
-    @pl.loop(0, KEY_VALUE_HEADS)
-    def _(h):
-        for j in range(HEADS_PER):
-            q_in(h, j).start()
-            g_in(h, j).start()
+    for table in tables:
+        table.start()
 
     barrier = pltpu.get_barrier_semaphore()
     for d in range(1, nx * nc):
@@ -126,65 +128,85 @@
             chosen = jnp.where(wide == at, table[at * SPAN : (at + 1) * SPAN, :], chosen)
         return chosen
 
-    for index, span in enumerate(spans):
+    def key_rotary(index):
         rows = slice(index * SPAN, (index + 1) * SPAN)
-        cosk[rows, :] = pick(span, cos_ref)
-        sink[rows, :] = pick(span, sin_ref)
-
-    @pl.loop(0, KEY_VALUE_HEADS)
-    def _(h):
+        cosk[rows, :] = pick(spans[index], cos_ref)
+        sink[rows, :] = pick(spans[index], sin_ref)
+
+    def to_across(s, h):
+        return pltpu.make_async_remote_copy(
+            kv.at[h, s, 0:TOK], kv.at[h, s, TOK : 2 * TOK], z_send.at[s, h], z_recv.at[s, h],
+            device_id=across, device_id_type=MESH,
+        )
+
+    def to_partner(s, h):
+        return pltpu.make_async_remote_copy(
+            kv.at[h, s, 0:TOK], kv.at[h, s, 2 * TOK : 3 * TOK], c_send.at[s, h], c_recv.at[s, h],
+            device_id=partner, device_id_type=MESH,
+        )
+
+    def forward(h):
+        return pltpu.make_async_remote_copy(
+            kv.at[h, :, TOK : 2 * TOK], kv.at[h, :, 3 * TOK : 4 * TOK], f_send.at[h], f_recv.at[h],
+            device_id=partner, device_id_type=MESH,
+        )
+
+    def grads_to_partner(h):
+        return pltpu.make_async_remote_copy(
+            sd.at[h], rd.at[h], d_send.at[h], d_recv.at[h],
+            device_id=partner, device_id_type=MESH,
+        )
+
+    def grads_across(h):
+        return pltpu.make_async_remote_copy(
+            si.at[h], ri.at[h], i_send.at[h], i_recv.at[h],
+            device_id=across, device_id_type=MESH,
+        )
+
+    def values_out(h):
+        v_in(h).wait()
+        to_across(1, h).start()
+        to_partner(1, h).start()
+
+    AHEAD = 2
+    pl.semaphore_wait(barrier, nx * nc - 1 + nz - 1)
+    for h in range(AHEAD):
+        values_out(h)
+
+    @pl.loop(0, KEY_VALUE_HEADS)
+    def _(h):
+        for j in range(HEADS_PER):
+            q_in(h, j).start()
+            g_in(h, j).start()
+
+    for h in range(KEY_VALUE_HEADS):
         k_in(h).wait()
-
     acc = jnp.zeros((TOK, HEAD_SIZE), F32)
     for h in range(KEY_VALUE_HEADS):
         x = k_vm[h].astype(F32)
         acc = acc + x * x
     mean_sq = jnp.sum(acc, axis=1, keepdims=True) * (1.0 / (KEY_VALUE_HEADS * HEAD_SIZE))
     rkb[...] = jnp.broadcast_to(lax.rsqrt(mean_sq + NORM_EPS), (TOK, HEAD_SIZE))
-
-    @pl.loop(0, KEY_VALUE_HEADS)
-    def _(h):
-        x = k_vm[h].astype(F32)
-        normed = x * rkb[...] * kg_ref[pl.ds(h, 1), :]
+    for table in tables:
+        table.wait()
+    key_rotary(0)
+    key_rotary(1)
+
+    @pl.loop(0, KEY_VALUE_HEADS)
+    def _(h):
+        normed = k_vm[h].astype(F32) * rkb[...] * kg_ref[pl.ds(h, 1), :]
         kv[h, 0, 0:TOK] = (normed * cosk[0:TOK] + swap_halves(normed) * sink[0:TOK]).astype(BF16)
-        v_in(h).wait()
-
-    pl.semaphore_wait(barrier, nx * nc - 1 + nz - 1)
-
-    def to_across(h):
-        return pltpu.make_async_remote_copy(
-            kv.at[h, :, 0:TOK], kv.at[h, :, TOK : 2 * TOK], z_send.at[h], z_recv.at[h],
-            device_id=across, device_id_type=MESH,
-        )
-
-    def to_partner(h):
-        return pltpu.make_async_remote_copy(
-            kv.at[h, :, 0:TOK], kv.at[h, :, 2 * TOK : 3 * TOK], c_send.at[h], c_recv.at[h],
-            device_id=partner, device_id_type=MESH,
-        )
-
-    def forward(h):
-        return pltpu.make_async_remote_copy(
-            kv.at[h, :, TOK : 2 * TOK], kv.at[h, :, 3 * TOK : 4 * TOK], f_send.at[h], f_recv.at[h],
-            device_id=partner, device_id_type=MESH,
-        )
-
-    def grads_to_partner(h):
-        return pltpu.make_async_remote_copy(
-            sd.at[h], rd.at[h], d_send.at[h], d_recv.at[h],
-            device_id=partner, device_id_type=MESH,
-        )
-
-    def grads_across(h):
-        return pltpu.make_async_remote_copy(
-            si.at[h], ri.at[h], i_send.at[h], i_recv.at[h],
-            device_id=across, device_id_type=MESH,
-        )
-
-    @pl.loop(0, KEY_VALUE_HEADS)
-    def _(h):
-        to_across(h).start()
-        to_partner(h).start()
+        to_across(0, h).start()
+        to_partner(0, h).start()
+
+        @pl.when(h < KEY_VALUE_HEADS - AHEAD)
+        def _():
+            values_out(h + AHEAD)
+
+    cq[...] = cosk[0:TOK] * SCALE
+    sq[...] = sink[0:TOK] * SCALE
+    for index in range(2, SPANS):
+        key_rotary(index)
 
     first = lane < SPAN
     query_span = jnp.where(first, spans[0], spans[1])
@@ -226,9 +248,21 @@
     rqb[...] = jnp.broadcast_to(lax.rsqrt(mean_sq + NORM_EPS), (TOK, HEAD_SIZE))
     inner[...] = jnp.zeros((TOK, HEAD_SIZE), F32)
 
-    z_take = to_across(0)
-    z_take.wait_recv()
-    forward(0).start()
+    def take(h):
+        to_across(0, h).wait_recv()
+        to_across(1, h).wait_recv()
+        forward(h).start()
+
+    @pl.loop(0, KEY_VALUE_HEADS)
+    def _(h):
+        for j in range(HEADS_PER):
+            rows = slice(j * TOK, (j + 1) * TOK)
+            normed = q_vm[h, rows].astype(F32) * rqb[...] * qg_ref[pl.ds(h * HEADS_PER + j, 1), :]
+            qr[h, rows] = (
+                normed * cosk[0:TOK] + swap_halves(normed) * sink[0:TOK]
+            ).astype(BF16)
+
+    take(0)
 
     def add_and_send(h):
         grads_to_partner(h).wait_recv()
@@ -242,36 +276,38 @@
     def _(h):
         @pl.when(h < KEY_VALUE_HEADS - 1)
         def _():
-            to_across(h + 1).wait_recv()
-            forward(h + 1).start()
-
-        for j in range(HEADS_PER):
-            x = q_vm[h, j * TOK : (j + 1) * TOK].astype(F32)
-            normed = x * rqb[...] * qg_ref[pl.ds(h * HEADS_PER + j, 1), :]
-            qr[j * TOK : (j + 1) * TOK] = (
-                normed * cosk[0:TOK] + swap_halves(normed) * sink[0:TOK]
-            ).astype(BF16)
-
-        to_partner(h).wait_recv()
+            take(h + 1)
+
+        to_partner(0, h).wait_recv()
+        to_partner(1, h).wait_recv()
         forward(h).wait_recv()
         nt = (((1,), (1,)), ((), ()))
-        st[...] = lax.dot_general(kv[h, 0], qr[...], nt, preferred_element_type=F32)
-        dp[...] = lax.dot_general(kv[h, 1], g_vm[h], nt, preferred_element_type=F32)
-
-        for j in range(HEADS_PER):
+        tn = (((0,), (0,)), ((), ()))
+        nn = (((1,), (0,)), ((), ()))
+
+        def scores(lo, hi):
+            part = slice(lo * TOK, hi * TOK)
+            raw = lax.dot_general(kv[h, 0], qr[h, part], nt, preferred_element_type=F32)
+            st[:, part] = raw
+            tops = []
+            for j in range(hi - lo):
+                cols = slice(j * TOK, (j + 1) * TOK)
+                top = jnp.full((8, TOK), -jnp.inf, F32)
+                for c in range(LENGTH // CH):
+                    rows = slice(c * CH, (c + 1) * CH)
+                    masked = raw[rows, cols] + bias[rows, :]
+                    top = jnp.maximum(top, jnp.max(masked.reshape(CH // 8, 8, TOK), axis=0))
+                tops.append(jnp.max(top, axis=0, keepdims=True) * SCALE2)
+            dp[:, part] = lax.dot_general(kv[h, 1], g_vm[h, part], nt, preferred_element_type=F32)
+            return tops
+
+        def softmax(j, top):
             cols = slice(j * TOK, (j + 1) * TOK)
-            top = jnp.full((8, TOK), -jnp.inf, F32)
-            for c in range(LENGTH // CH):
-                rows = slice(c * CH, (c + 1) * CH)
-                s = st[rows, cols] * SCALE2 + bias[rows, :]
-                st[rows, cols] = s
-                top = jnp.maximum(top, jnp.max(s.reshape(CH // 8, 8, TOK), axis=0))
-            top = jnp.max(top, axis=0, keepdims=True)
             weight = jnp.zeros((8, TOK), F32)
             delta = jnp.zeros((8, TOK), F32)
             for c in range(LENGTH // CH):
                 rows = slice(c * CH, (c + 1) * CH)
-                p = jnp.exp2(st[rows, cols] - top)
+                p = jnp.exp2((st[rows, cols] + bias[rows, :]) * SCALE2 - top)
                 st[rows, cols] = p
                 weight = weight + jnp.sum(p.reshape(CH // 8, 8, TOK), axis=0)
                 delta = delta + jnp.sum((p * dp[rows, cols]).reshape(CH // 8, 8, TOK), axis=0)
@@ -283,23 +319,33 @@
                 pt[rows, cols] = p.astype(BF16)
                 ds[rows, cols] = (p * (dp[rows, cols] - delta)).astype(BF16)
 
-        tn = (((0,), (0,)), ((), ()))
-        dq = lax.dot_general(ds[...], kv[h, 0], tn, preferred_element_type=F32)
-        for j in range(HEADS_PER):
-            part = dq[j * TOK : (j + 1) * TOK] * SCALE
-            part = part * cosk[0:TOK] - swap_halves(part) * sink[0:TOK]
-            x = q_vm[h, j * TOK : (j + 1) * TOK].astype(F32)
-            gpart[h, j : j + 1, :] = jnp.sum(part * x * rqb[...], axis=0, keepdims=True)
-            weighted = part * qg_ref[pl.ds(h * HEADS_PER + j, 1), :]
-            dqw[h, j * TOK : (j + 1) * TOK] = weighted
-            inner[...] = inner[...] + weighted * x
-
-        nn = (((1,), (0,)), ((), ()))
-        dv = lax.dot_general(pt[...], g_vm[h], nn, preferred_element_type=F32)
+        def query_grads(lo, hi):
+            part = slice(lo * TOK, hi * TOK)
+            dq = lax.dot_general(ds[:, part], kv[h, 0], tn, preferred_element_type=F32)
+            along = jnp.zeros((TOK, HEAD_SIZE), F32)
+            for j in range(lo, hi):
+                d_part = dq[(j - lo) * TOK : (j - lo + 1) * TOK]
+                d_part = d_part * cq[...] - swap_halves(d_part) * sq[...]
+                dqw[h, j * TOK : (j + 1) * TOK] = d_part
+                d_part = d_part * q_vm[h, j * TOK : (j + 1) * TOK].astype(F32)
+                gpart[h, j : j + 1, :] = jnp.sum(d_part * rqb[...], axis=0, keepdims=True)
+                along = along + d_part * qg_ref[pl.ds(h * HEADS_PER + j, 1), :]
+            inner[...] = inner[...] + along
+
+        def key_grads(lo, hi):
+            part = slice(lo * TOK, hi * TOK)
+            dv = lax.dot_general(pt[:, part], g_vm[h, part], nn, preferred_element_type=F32)
+            dk = lax.dot_general(ds[:, part], qr[h, part], nn, preferred_element_type=F32)
+            return dk, dv
+
+        tops = scores(0, 2) + scores(2, 4) + scores(4, 5)
+        for j in range(HEADS_PER):
+            softmax(j, tops[j])
+        query_grads(0, HEADS_PER)
+        dk, dv = key_grads(0, HEADS_PER)
         own[h, 1] = dv[0:TOK]
         mid[h, 1] = dv[TOK : 2 * TOK]
         sd[h, 1] = dv[2 * TOK :]
-        dk = lax.dot_general(ds[...], qr[...], nn, preferred_element_type=F32) * SCALE
         own[h, 0] = dk[0:TOK]
         mid[h, 0] = dk[TOK : 2 * TOK]
         sd[h, 0] = dk[2 * TOK :]
@@ -314,7 +360,7 @@
             k_part = k_part * cosk[rows] - swap_halves(k_part) * sink[rows]
             total = total + jnp.sum((d_part * k_part).reshape(TOK // 8, 8, HEAD_SIZE), axis=0)
         gpart[h, HEADS_PER : HEADS_PER + 1, :] = (
-            jnp.sum(total, axis=0, keepdims=True) / kg_ref[pl.ds(h, 1), :]
+            jnp.sum(total, axis=0, keepdims=True) * SCALE / kg_ref[pl.ds(h, 1), :]
         )
         gpart[h, HEADS_PER + 1 :, :] = jnp.zeros((7 - HEADS_PER, HEAD_SIZE), F32)
 
@@ -383,7 +429,8 @@
         for j in range(HEADS_PER):
             rows = slice(j * TOK, (j + 1) * TOK)
             x = q_vm[h, rows].astype(F32)
-            outb[h, rows] = (rqb[...] * dqw[h, rows] - x * inner[...]).astype(BF16)
+            weighted = dqw[h, rows] * qg_ref[pl.ds(h * HEADS_PER + j, 1), :]
+            outb[h, rows] = (rqb[...] * weighted - x * inner[...]).astype(BF16)
             q_out(h, j).start()
 
     for d in range(1, nz):
@@ -405,7 +452,7 @@
     def _(h):
         grads_across(h).wait()
         d_part = own[h, 0] + rd[h, 0, 0:TOK] + ri[h, 0].astype(F32)
-        d_part = d_part * cosk[0:TOK] - swap_halves(d_part) * sink[0:TOK]
+        d_part = d_part * cq[...] - swap_halves(d_part) * sq[...]
         weighted = d_part * kg_ref[pl.ds(h, 1), :]
         dkw[h] = weighted
         inner[...] = inner[...] + weighted * k_vm[h].astype(F32)
@@ -428,8 +475,9 @@
 
     @pl.loop(0, KEY_VALUE_HEADS)
     def _(h):
-        to_across(h).wait_send()
-        to_partner(h).wait_send()
+        for s in range(2):
+            to_across(s, h).wait_send()
+            to_partner(s, h).wait_send()
         forward(h).wait_send()
         grads_to_partner(h).wait_send()
         for j in range(HEADS_PER):
@@ -442,6 +490,16 @@
         total_out(d).wait_send()
     for d in range(1, nz):
         z_out(d).wait_send()
+
+
+def settle(*refs):
+    copies = [
+        pltpu.make_async_copy(refs[i], refs[5 + i], refs[10].at[i]) for i in range(5)
+    ]
+    for copy in copies:
+        copy.start()
+    for copy in copies:
+        copy.wait()
 
 
 def body(nx, nz, nc, query_proj, key_proj, values, grad_out, query_gain, key_gain, segments, layout):
@@ -460,14 +518,17 @@
             jax.ShapeDtypeStruct((QUERY_HEADS, hs), F32),
             jax.ShapeDtypeStruct((kvh, hs), F32),
         ),
-        in_specs=[any_spec] * 4 + [vm_spec] * 5 + [pl.BlockSpec(memory_space=pltpu.SMEM)],
+        in_specs=[pl.BlockSpec(memory_space=pltpu.HBM)] * 7 + [vm_spec] * 2 + [pl.BlockSpec(memory_space=pltpu.SMEM)],
         out_specs=(any_spec, any_spec, any_spec, vm_spec, vm_spec),
         scratch_shapes=[
+            pltpu.VMEM((LENGTH, hs), F32),
+            pltpu.VMEM((LENGTH, hs), F32),
+            pltpu.VMEM((segments.shape[0] // TOK, TOK), jnp.int32),
             pltpu.VMEM((kvh, QROWS, hs), BF16),
             pltpu.VMEM((kvh, QROWS, hs), BF16),
             pltpu.VMEM((kvh, TOK, hs), BF16),
             pltpu.VMEM((kvh, 2, LENGTH, hs), BF16),
-            pltpu.VMEM((QROWS, hs), BF16),
+            pltpu.VMEM((kvh, QROWS, hs), BF16),
             pltpu.VMEM((LENGTH, QROWS), F32),
             pltpu.VMEM((LENGTH, QROWS), F32),
             pltpu.VMEM((LENGTH, QROWS), BF16),
@@ -478,6 +539,8 @@
             pltpu.VMEM((LENGTH, TOK), F32),
             pltpu.VMEM((LENGTH, hs), F32),
             pltpu.VMEM((LENGTH, hs), F32),
+            pltpu.VMEM((TOK, hs), F32),
+            pltpu.VMEM((TOK, hs), F32),
             pltpu.VMEM((TOK, hs), F32),
             pltpu.VMEM((TOK, hs), F32),
             pltpu.VMEM((TOK, hs), F32),
@@ -492,20 +555,33 @@
             pltpu.VMEM((nx * nc, 8, hs), F32),
             pltpu.VMEM((nz, 8, hs), F32),
             pltpu.VMEM((kvh, 8, hs), F32),
-            dma((2, kvh, HEADS_PER)), dma((kvh,)), dma((kvh,)),
-            dma((kvh,)), dma((kvh,)), dma((kvh,)), dma((kvh,)), dma((kvh,)), dma((kvh,)),
+            dma((2, kvh, HEADS_PER)), dma((kvh,)), dma((kvh,)), dma((3,)),
+            dma((2, kvh)), dma((2, kvh)), dma((2, kvh)), dma((2, kvh)), dma((kvh,)), dma((kvh,)),
             dma((kvh,)), dma((kvh,)), dma((kvh,)), dma((kvh,)),
             dma((nx * nc,)), dma((nx * nc,)), dma((nz,)), dma((nz,)), dma((kvh,)), dma((kvh,)),
             dma((kvh, HEADS_PER + 2)),
         ],
         compiler_params=pltpu.CompilerParams(
-            collective_id=0, has_side_effects=True, vmem_limit_bytes=56 * 1024 * 1024
+            collective_id=0, has_side_effects=True, vmem_limit_bytes=36 * 1024 * 1024
         ),
     )(
-        query_proj, key_proj, values, grad_out,
-        query_gain.reshape(QUERY_HEADS, hs), key_gain.reshape(kvh, hs),
-        segments.reshape(-1, TOK), jnp.asarray(cos_table), jnp.asarray(sin_table), layout,
+        *(
+            pltpu.with_memory_space_constraint(x, pltpu.HBM)
+            for x in (
+                query_proj, key_proj, values, grad_out,
+                jnp.asarray(cos_table), jnp.asarray(sin_table), segments.reshape(-1, TOK),
+                query_gain.reshape(QUERY_HEADS, hs), key_gain.reshape(kvh, hs), layout,
+            )
+        ),
     )
+    out = pl.pallas_call(
+        settle,
+        out_shape=[jax.ShapeDtypeStruct(o.shape, o.dtype) for o in out],
+        in_specs=[any_spec] * 5,
+        out_specs=[any_spec] * 5,
+        scratch_shapes=[dma((5,))],
+        compiler_params=pltpu.CompilerParams(vmem_limit_bytes=1024 * 1024),
+    )(*out)
     return out[0], out[1], out[2], out[3].reshape(-1), out[4].reshape(-1)
 
 

time: 75.1 us -> 69.4 us (0.924)
  local copies, waits for them, and re-layouts: 5.13 us -> 0 us
    unnamed x13 -> x0, local copies, waits for them, and re-layouts: 5.13 us -> none
    pallas_call x1, Pallas kernels: 69.1 us -> 67.3 us  [body(): pl.pallas_call(functools.partial(kernel, nx, nz, nc), out_shape=(jax.Shap...]
    pallas_call x0 -> x1, Pallas kernels: none -> 1.27 us  [body(): pl.pallas_call(settle, out_shape=[jax.ShapeDtypeStruct(o.shape, o.dtype)...]
where the time goes in v2:
time: 69.4 us; the launch traced here: 69.2 us
  Pallas kernels  68.6 us (99%)
    pallas_call x1, Pallas kernels, body(): pl.pallas_call(functools.partial(kernel, nx, nz, nc), out_shape=(jax.Shap...  67.3 us

profile of v2, /device:TPU:33, one launch (start us, length us, event | category | flops | bytes accessed | tf_op | source)
XLA Modules:
  0.0 69.2 jit_solution(14026972349877635352)
XLA Ops:
  0.6 67.3 %shard_map.137 = (bf16[128,5120]{1,0:T(8,128)(2,1)S(1)}, bf16[128,1024]{1,0:T(8,128)(2,1)S(1)}, bf16[128,1024]{1,0:T(8,128)(2,1)S(1)}, f32[40,128]{1,0:T(8,128)S(1)}, f32[8,128]{1,0:T(8,128)S(1)}) custom-call(bf16[128,5120]{1,0:T(8,128)(2,1)} %q_hbm.1, bf16[128,1024]{1,0:T(8,128)(2,1)} %k_hbm.1, bf16[128,1024]{1,0:T(8,128)(2,1)} %v_hbm.1, ...), custom_call_target="tpu_custom_call" | custom-call | tf_op jit(solution)/shard_map/pallas_call | solution.py:512
  68.0 1.3 %shard_map.138 = (bf16[128,5120]{1,0:T(8,128)(2,1)}, bf16[128,1024]{1,0:T(8,128)(2,1)}, bf16[128,1024]{1,0:T(8,128)(2,1)}, f32[40,128]{1,0:T(8,128)}, f32[8,128]{1,0:T(8,128)}) custom-call(bf16[128,5120]{1,0:T(8,128)(2,1)S(1)} %get-tuple-element.15.refs_0_, bf16[128,1024]{1,0:T(8,128)(2,1)S(1)} %get-tuple-element.16.refs_1_, ...), custom_call_target="tpu_custom_call" | custom-call | tf_op jit(solution)/shard_map/pallas_call | solution.py:577

commit v3 on v2

--- a/solution.py
+++ b/solution.py
@@ -21,6 +21,8 @@
 QROWS = HEADS_PER * TOK
 CONTEXT = ("context_0", "context_1", "context_2")
 GROUPS_CONTEXT = ("groups", "context_0", "context_1", "context_2")
+LATE = 2
+EARLY = KEY_VALUE_HEADS - LATE
 NORM_EPS = 1e-06
 ROPE_BASE = 500000.0
 SCALE = HEAD_SIZE ** (-0.5)
@@ -50,14 +52,15 @@
     q_hbm, k_hbm, v_hbm, g_hbm, cos_hbm, sin_hbm, seg_hbm, qg_ref, kg_ref, lay_ref,
     qgrad_hbm, kgrad_hbm, vgrad_hbm, qgain_ref, kgain_ref,
     cos_ref, sin_ref, seg_ref,
-    q_vm, g_vm, k_vm, kv, qr, st, dp, pt, ds, dqw, dkw,
+    q_vm, g_vm, k_vm, kv, qr, st0, st1, dp0, dp1, pt, ds, dqw, dkw,
     bias, segcol, cosk, sink, cq, sq, rqb, rkb, inner,
     own, mid, sd, rd, si, ri, outb,
-    gpart, rs, zb, ag,
+    tops0, tops1, gpart, rs, pf, za, zf, ag,
     in_sem, kin_sem, vin_sem, tab_sem,
     z_send, z_recv, c_send, c_recv, f_send, f_recv,
     d_send, d_recv, i_send, i_recv,
-    rs_send, rs_recv, zb_send, zb_recv, ag_send, ag_recv, out_sem,
+    rs_send, rs_recv, pf_send, pf_recv, za_send, za_recv, zf_send, zf_recv, ag_send, ag_recv,
+    out_sem,
 ):
     xi = lax.axis_index("context_0")
     zi = lax.axis_index("context_1")
@@ -73,7 +76,7 @@
 
     def k_in(h):
         cols = pl.ds(pl.multiple_of(h * HEAD_SIZE, HEAD_SIZE), HEAD_SIZE)
-        return pltpu.make_async_copy(k_hbm.at[:, cols], k_vm.at[h], kin_sem.at[h])
+        return pltpu.make_async_copy(k_hbm.at[:, cols], k_vm.at[h], kin_sem.at[0])
 
     def v_in(h):
         cols = pl.ds(pl.multiple_of(h * HEAD_SIZE, HEAD_SIZE), HEAD_SIZE)
@@ -82,12 +85,12 @@
     def q_in(h, j):
         cols = pl.ds(pl.multiple_of((h * HEADS_PER + j) * HEAD_SIZE, HEAD_SIZE), HEAD_SIZE)
         rows = pl.ds(j * TOK, TOK)
-        return pltpu.make_async_copy(q_hbm.at[:, cols], q_vm.at[h, rows], in_sem.at[0, h, j])
+        return pltpu.make_async_copy(q_hbm.at[:, cols], q_vm.at[h, rows], kin_sem.at[1])
 
     def g_in(h, j):
         cols = pl.ds(pl.multiple_of((h * HEADS_PER + j) * HEAD_SIZE, HEAD_SIZE), HEAD_SIZE)
         rows = pl.ds(j * TOK, TOK)
-        return pltpu.make_async_copy(g_hbm.at[:, cols], g_vm.at[h, rows], in_sem.at[1, h, j])
+        return pltpu.make_async_copy(g_hbm.at[:, cols], g_vm.at[h, rows], in_sem.at[h])
 
     tables = [
         pltpu.make_async_copy(source, target, tab_sem.at[index])
@@ -179,8 +182,7 @@
             q_in(h, j).start()
             g_in(h, j).start()
 
-    for h in range(KEY_VALUE_HEADS):
-        k_in(h).wait()
+    pltpu.make_async_copy(k_vm, k_vm, kin_sem.at[0]).wait()
     acc = jnp.zeros((TOK, HEAD_SIZE), F32)
     for h in range(KEY_VALUE_HEADS):
         x = k_vm[h].astype(F32)
@@ -228,12 +230,7 @@
         allowed = (doc_col == doc_row) & (pos_col <= pos_row)
         bias[index * SPAN : (index + 1) * SPAN, :] = jnp.where(allowed, 0.0, -jnp.inf)
 
-    @pl.loop(0, KEY_VALUE_HEADS)
-    def _(h):
-        for j in range(HEADS_PER):
-            q_in(h, j).wait()
-            g_in(h, j).wait()
-
+    pltpu.make_async_copy(q_vm, q_vm, kin_sem.at[1]).wait()
     inner[...] = jnp.zeros((TOK, HEAD_SIZE), F32)
 
     @pl.loop(0, KEY_VALUE_HEADS)
@@ -262,95 +259,151 @@
                 normed * cosk[0:TOK] + swap_halves(normed) * sink[0:TOK]
             ).astype(BF16)
 
-    take(0)
-
     def add_and_send(h):
         grads_to_partner(h).wait_recv()
         for s in range(2):
             si[h, s] = (mid[h, s] + rd[h, s, TOK : 2 * TOK]).astype(BF16)
         grads_across(h).start()
 
+    def shard_out(h):
+        return pltpu.make_async_remote_copy(
+            gpart.at[h], rs.at[rank], rs_send.at[h], rs_recv.at[rank],
+            device_id=rank_peer(h), device_id_type=MESH,
+        )
+
+    def shard_got(source):
+        return pltpu.make_async_remote_copy(
+            gpart.at[0], rs.at[source], rs_send.at[0], rs_recv.at[source],
+            device_id=rank_peer(source), device_id_type=MESH,
+        )
+
+    def plane_out(late, d):
+        other = jnp.bitwise_xor(rank, d)
+        return pltpu.make_async_remote_copy(
+            gpart.at[EARLY + late], pf.at[late, rank], pf_send.at[late, d], pf_recv.at[late, rank],
+            device_id=rank_peer(other), device_id_type=MESH,
+        )
+
+    def plane_got(late, d):
+        other = jnp.bitwise_xor(rank, d)
+        return pltpu.make_async_remote_copy(
+            gpart.at[EARLY + late], pf.at[late, other], pf_send.at[late, d], pf_recv.at[late, other],
+            device_id=rank_peer(other), device_id_type=MESH,
+        )
+
+    def z_copy(buffer, send, recv, d, source):
+        return pltpu.make_async_remote_copy(
+            buffer.at[source], buffer.at[source], send.at[d], recv.at[source],
+            device_id={"context_1": lax.rem(zi + d, nz)}, device_id_type=MESH,
+        )
+
+    def z_out(d):
+        return z_copy(za, za_send, za_recv, d, zi)
+
+    def z_got(d):
+        return z_copy(za, za_send, za_recv, d, lax.rem(zi + d, nz))
+
+    def late_out(d):
+        return z_copy(zf, zf_send, zf_recv, d, zi)
+
+    def late_got(d):
+        return z_copy(zf, zf_send, zf_recv, d, lax.rem(zi + d, nz))
+
+    def total_out(d):
+        other = jnp.bitwise_xor(rank, d)
+        return pltpu.make_async_remote_copy(
+            ag.at[rank], ag.at[rank], ag_send.at[d], ag_recv.at[rank],
+            device_id=rank_peer(other), device_id_type=MESH,
+        )
+
+    def total_got(source):
+        return pltpu.make_async_remote_copy(
+            ag.at[source], ag.at[source], ag_send.at[0], ag_recv.at[source],
+            device_id=rank_peer(source), device_id_type=MESH,
+        )
+
+    far_first = sorted(range(1, nz), key=lambda d: -min(d, nz - d))
+    owner = rank < EARLY
+
+    def shards_over_z():
+        @pl.when(owner)
+        def _():
+            rs[rank] = gpart[rank]
+            for d in range(1, nx * nc):
+                shard_got(jnp.bitwise_xor(rank, d)).wait_recv()
+            za[zi] = jnp.sum(rs[...], axis=0)
+            for d in far_first:
+                z_out(d).start()
+
     CH = 64
-
-    @pl.loop(0, KEY_VALUE_HEADS)
-    def _(h):
-        @pl.when(h < KEY_VALUE_HEADS - 1)
-        def _():
-            take(h + 1)
-
+    nt = (((1,), (1,)), ((), ()))
+    tn = (((0,), (0,)), ((), ()))
+    nn = (((1,), (0,)), ((), ()))
+
+    def arrived(h):
         to_partner(0, h).wait_recv()
         to_partner(1, h).wait_recv()
         forward(h).wait_recv()
-        nt = (((1,), (1,)), ((), ()))
-        tn = (((0,), (0,)), ((), ()))
-        nn = (((1,), (0,)), ((), ()))
-
-        def scores(lo, hi):
+        pltpu.make_async_copy(g_vm.at[h], g_vm.at[h], in_sem.at[h]).wait()
+
+    slots = ((st0, dp0, tops0), (st1, dp1, tops1))
+
+    PARTS = ((0, 2), (2, 4), (4, 5))
+
+    def scores(h, slot, parts=PARTS):
+        st, dp, tops = slots[slot]
+        for lo, hi in parts:
             part = slice(lo * TOK, hi * TOK)
             raw = lax.dot_general(kv[h, 0], qr[h, part], nt, preferred_element_type=F32)
             st[:, part] = raw
-            tops = []
-            for j in range(hi - lo):
-                cols = slice(j * TOK, (j + 1) * TOK)
+            for j in range(lo, hi):
+                cols = slice((j - lo) * TOK, (j - lo + 1) * TOK)
                 top = jnp.full((8, TOK), -jnp.inf, F32)
                 for c in range(LENGTH // CH):
                     rows = slice(c * CH, (c + 1) * CH)
                     masked = raw[rows, cols] + bias[rows, :]
                     top = jnp.maximum(top, jnp.max(masked.reshape(CH // 8, 8, TOK), axis=0))
-                tops.append(jnp.max(top, axis=0, keepdims=True) * SCALE2)
+                tops[j : j + 1, :] = jnp.max(top, axis=0, keepdims=True) * SCALE2
             dp[:, part] = lax.dot_general(kv[h, 1], g_vm[h, part], nt, preferred_element_type=F32)
-            return tops
-
-        def softmax(j, top):
-            cols = slice(j * TOK, (j + 1) * TOK)
-            weight = jnp.zeros((8, TOK), F32)
-            delta = jnp.zeros((8, TOK), F32)
-            for c in range(LENGTH // CH):
-                rows = slice(c * CH, (c + 1) * CH)
-                p = jnp.exp2((st[rows, cols] + bias[rows, :]) * SCALE2 - top)
-                st[rows, cols] = p
-                weight = weight + jnp.sum(p.reshape(CH // 8, 8, TOK), axis=0)
-                delta = delta + jnp.sum((p * dp[rows, cols]).reshape(CH // 8, 8, TOK), axis=0)
-            norm = 1.0 / jnp.sum(weight, axis=0, keepdims=True)
-            delta = jnp.sum(delta, axis=0, keepdims=True) * norm
-            for c in range(LENGTH // CH):
-                rows = slice(c * CH, (c + 1) * CH)
-                p = st[rows, cols] * norm
-                pt[rows, cols] = p.astype(BF16)
-                ds[rows, cols] = (p * (dp[rows, cols] - delta)).astype(BF16)
-
-        def query_grads(lo, hi):
-            part = slice(lo * TOK, hi * TOK)
-            dq = lax.dot_general(ds[:, part], kv[h, 0], tn, preferred_element_type=F32)
-            along = jnp.zeros((TOK, HEAD_SIZE), F32)
-            for j in range(lo, hi):
-                d_part = dq[(j - lo) * TOK : (j - lo + 1) * TOK]
-                d_part = d_part * cq[...] - swap_halves(d_part) * sq[...]
-                dqw[h, j * TOK : (j + 1) * TOK] = d_part
-                d_part = d_part * q_vm[h, j * TOK : (j + 1) * TOK].astype(F32)
-                gpart[h, j : j + 1, :] = jnp.sum(d_part * rqb[...], axis=0, keepdims=True)
-                along = along + d_part * qg_ref[pl.ds(h * HEADS_PER + j, 1), :]
-            inner[...] = inner[...] + along
-
-        def key_grads(lo, hi):
-            part = slice(lo * TOK, hi * TOK)
-            dv = lax.dot_general(pt[:, part], g_vm[h, part], nn, preferred_element_type=F32)
-            dk = lax.dot_general(ds[:, part], qr[h, part], nn, preferred_element_type=F32)
-            return dk, dv
-
-        tops = scores(0, 2) + scores(2, 4) + scores(4, 5)
+
+    def softmax(j, slot):
+        st, dp, tops = slots[slot]
+        cols = slice(j * TOK, (j + 1) * TOK)
+        top = tops[j : j + 1, :]
+        weight = jnp.zeros((8, TOK), F32)
+        delta = jnp.zeros((8, TOK), F32)
+        for c in range(LENGTH // CH):
+            rows = slice(c * CH, (c + 1) * CH)
+            p = jnp.exp2((st[rows, cols] + bias[rows, :]) * SCALE2 - top)
+            st[rows, cols] = p
+            weight = weight + jnp.sum(p.reshape(CH // 8, 8, TOK), axis=0)
+            delta = delta + jnp.sum((p * dp[rows, cols]).reshape(CH // 8, 8, TOK), axis=0)
+        norm = 1.0 / jnp.sum(weight, axis=0, keepdims=True)
+        delta = jnp.sum(delta, axis=0, keepdims=True) * norm
+        for c in range(LENGTH // CH):
+            rows = slice(c * CH, (c + 1) * CH)
+            p = st[rows, cols] * norm
+            pt[rows, cols] = p.astype(BF16)
+            ds[rows, cols] = (p * (dp[rows, cols] - delta)).astype(BF16)
+
+    def query_grads(h):
+        dq = lax.dot_general(ds[...], kv[h, 0], tn, preferred_element_type=F32)
+        along = jnp.zeros((TOK, HEAD_SIZE), F32)
         for j in range(HEADS_PER):
-            softmax(j, tops[j])
-        query_grads(0, HEADS_PER)
-        dk, dv = key_grads(0, HEADS_PER)
-        own[h, 1] = dv[0:TOK]
-        mid[h, 1] = dv[TOK : 2 * TOK]
-        sd[h, 1] = dv[2 * TOK :]
+            d_part = dq[j * TOK : (j + 1) * TOK]
+            d_part = d_part * cq[...] - swap_halves(d_part) * sq[...]
+            dqw[h, j * TOK : (j + 1) * TOK] = d_part
+            d_part = d_part * q_vm[h, j * TOK : (j + 1) * TOK].astype(F32)
+            gpart[h, j : j + 1, :] = jnp.sum(d_part * rqb[...], axis=0, keepdims=True)
+            along = along + d_part * qg_ref[pl.ds(h * HEADS_PER + j, 1), :]
+        inner[...] = inner[...] + along
+
+    def key_grads(h):
+        dk = lax.dot_general(ds[...], qr[h], nn, preferred_element_type=F32)
+        dv = lax.dot_general(pt[...], g_vm[h], nn, preferred_element_type=F32)
         own[h, 0] = dk[0:TOK]
         mid[h, 0] = dk[TOK : 2 * TOK]
         sd[h, 0] = dk[2 * TOK :]
-        grads_to_partner(h).start()
-
         total = jnp.zeros((8, HEAD_SIZE), F32)
         for c in range(4):
             rows = slice(c * TOK, (c + 1) * TOK)
@@ -364,56 +417,63 @@
         )
         gpart[h, HEADS_PER + 1 :, :] = jnp.zeros((7 - HEADS_PER, HEAD_SIZE), F32)
 
-        @pl.when(h > 0)
-        def _():
-            add_and_send(h - 1)
-
-    def shard_out(d):
-        other = jnp.bitwise_xor(rank, d)
-        return pltpu.make_async_remote_copy(
-            gpart.at[other], rs.at[d], rs_send.at[d], rs_recv.at[d],
-            device_id=rank_peer(other), device_id_type=MESH,
-        )
-
-    def z_out(d):
-        return pltpu.make_async_remote_copy(
-            zb.at[zi], zb.at[zi], zb_send.at[d], zb_recv.at[zi],
-            device_id={"context_1": lax.rem(zi + d, nz)}, device_id_type=MESH,
-        )
-
-    def z_got(d):
-        source = lax.rem(zi + d, nz)
-        return pltpu.make_async_remote_copy(
-            zb.at[source], zb.at[source], zb_send.at[d], zb_recv.at[source],
-            device_id={"context_1": source}, device_id_type=MESH,
-        )
-
-    def total_out(d):
-        other = jnp.bitwise_xor(rank, d)
-        return pltpu.make_async_remote_copy(
-            ag.at[rank], ag.at[rank], ag_send.at[d], ag_recv.at[rank],
-            device_id=rank_peer(other), device_id_type=MESH,
-        )
-
-    def total_got(d):
-        other = jnp.bitwise_xor(rank, d)
-        return pltpu.make_async_remote_copy(
-            ag.at[other], ag.at[other], ag_send.at[d], ag_recv.at[other],
-            device_id=rank_peer(other), device_id_type=MESH,
-        )
-
-    for d in range(1, nx * nc):
-        shard_out(d).start()
-
-    add_and_send(KEY_VALUE_HEADS - 1)
-
-    summed = gpart[rank]
-    for d in range(1, nx * nc):
-        shard_out(d).wait_recv()
-        summed = summed + rs[d]
-    zb[zi] = summed
-    for d in range(1, nz):
-        z_out(d).start()
+        own[h, 1] = dv[0:TOK]
+        mid[h, 1] = dv[TOK : 2 * TOK]
+        sd[h, 1] = dv[2 * TOK :]
+
+    def step(h, slot, first=None, last=False):
+        if first is None:
+            add_and_send(h - 2)
+        else:
+            @pl.when(jnp.logical_not(first))
+            def _():
+                add_and_send(h - 2)
+
+        if not last:
+            arrived(h + 1)
+            if not isinstance(h, int):
+                take(h + 2)
+        for lo, hi in PARTS:
+            if not last:
+                scores(h + 1, 1 - slot, ((lo, hi),))
+            for j in range(lo, hi):
+                softmax(j, slot)
+        query_grads(h)
+        key_grads(h)
+        if isinstance(h, int):
+            for d in range(1, nx * nc):
+                plane_out(h - EARLY, d).start()
+        else:
+            @pl.when(rank != h)
+            def _():
+                shard_out(h).start()
+
+        grads_to_partner(h).start()
+
+    for h in range(2):
+        take(h)
+    arrived(0)
+    scores(0, 0)
+
+    @pl.loop(0, EARLY // 2)
+    def _(i):
+        step(2 * i, 0, first=i == 0)
+        step(2 * i + 1, 1, first=i == 0)
+
+    last = KEY_VALUE_HEADS - 1
+    step(last - 1, 0)
+    step(last, 1, last=True)
+    add_and_send(last - 1)
+    shards_over_z()
+
+    for late in range(LATE):
+        pf[late, rank] = gpart[EARLY + late]
+        for d in range(1, nx * nc):
+            plane_got(late, d).wait_recv()
+        zf[zi, late] = jnp.sum(pf[late], axis=0)
+    for d in far_first:
+        late_out(d).start()
+    add_and_send(last)
 
     inner_q = jnp.sum(inner[...], axis=1, keepdims=True) * (1.0 / (QUERY_HEADS * HEAD_SIZE))
     cube = rqb[...] * rqb[...] * rqb[...] * inner_q
@@ -433,14 +493,13 @@
             outb[h, rows] = (rqb[...] * weighted - x * inner[...]).astype(BF16)
             q_out(h, j).start()
 
-    for d in range(1, nz):
-        z_got(d).wait_recv()
-    total = zb[0]
-    for d in range(1, nz):
-        total = total + zb[d]
-    ag[rank] = total
-    for d in range(1, nx * nc):
-        total_out(d).start()
+    @pl.when(owner)
+    def _():
+        for d in range(1, nz):
+            z_got(d).wait_recv()
+        ag[rank] = jnp.sum(za[...], axis=0)
+        for d in range(1, nx * nc):
+            total_out(d).start()
 
     def k_out(h, s, out):
         cols = pl.ds(pl.multiple_of(h * HEAD_SIZE, HEAD_SIZE), HEAD_SIZE)
@@ -467,11 +526,17 @@
         si[h, 0] = (rkb[...] * dkw[h] - k_vm[h].astype(F32) * inner[...]).astype(BF16)
         k_out(h, 0, kgrad_hbm).start()
 
-    for d in range(1, nx * nc):
-        total_got(d).wait_recv()
+    for d in range(1, nz):
+        late_got(d).wait_recv()
+    late_totals = jnp.sum(zf[...], axis=0)
+    for source in range(EARLY):
+        @pl.when(rank != source)
+        def _():
+            total_got(source).wait_recv()
     for h in range(KEY_VALUE_HEADS):
-        qgain_ref[h * HEADS_PER : (h + 1) * HEADS_PER, :] = ag[h, 0:HEADS_PER, :]
-        kgain_ref[h : h + 1, :] = ag[h, HEADS_PER : HEADS_PER + 1, :]
+        total = ag[h] if h < EARLY else late_totals[h - EARLY]
+        qgain_ref[h * HEADS_PER : (h + 1) * HEADS_PER, :] = total[0:HEADS_PER, :]
+        kgain_ref[h : h + 1, :] = total[HEADS_PER : HEADS_PER + 1, :]
 
     @pl.loop(0, KEY_VALUE_HEADS)
     def _(h):
@@ -485,11 +550,22 @@
         k_out(h, 0, kgrad_hbm).wait()
         k_out(h, 1, vgrad_hbm).wait()
 
+    for h in range(EARLY):
+        @pl.when(rank != h)
+        def _():
+            shard_out(h).wait_send()
     for d in range(1, nx * nc):
-        shard_out(d).wait_send()
-        total_out(d).wait_send()
+        for late in range(LATE):
+            plane_out(late, d).wait_send()
     for d in range(1, nz):
-        z_out(d).wait_send()
+        late_out(d).wait_send()
+
+    @pl.when(owner)
+    def _():
+        for d in range(1, nx * nc):
+            total_out(d).wait_send()
+        for d in range(1, nz):
+            z_out(d).wait_send()
 
 
 def settle(*refs):
@@ -504,7 +580,7 @@
 
 def body(nx, nz, nc, query_proj, key_proj, values, grad_out, query_gain, key_gain, segments, layout):
     cos_table, sin_table = rope_tables()
-    assert nx * nc == KEY_VALUE_HEADS or nx * nc < KEY_VALUE_HEADS
+    assert nx * nc == KEY_VALUE_HEADS
     kvh, hs = KEY_VALUE_HEADS, HEAD_SIZE
     any_spec = pl.BlockSpec(memory_space=pl.ANY)
     vm_spec = pl.BlockSpec(memory_space=pltpu.VMEM)
@@ -531,6 +607,8 @@
             pltpu.VMEM((kvh, QROWS, hs), BF16),
             pltpu.VMEM((LENGTH, QROWS), F32),
             pltpu.VMEM((LENGTH, QROWS), F32),
+            pltpu.VMEM((LENGTH, QROWS), F32),
+            pltpu.VMEM((LENGTH, QROWS), F32),
             pltpu.VMEM((LENGTH, QROWS), BF16),
             pltpu.VMEM((LENGTH, QROWS), BF16),
             pltpu.VMEM((kvh, QROWS, hs), F32),
@@ -551,14 +629,19 @@
             pltpu.VMEM((kvh, 2, TOK, hs), BF16),
             pltpu.VMEM((kvh, 2, TOK, hs), BF16),
             pltpu.VMEM((kvh, QROWS, hs), BF16),
+            pltpu.VMEM((8, TOK), F32),
+            pltpu.VMEM((8, TOK), F32),
             pltpu.VMEM((kvh, 8, hs), F32),
-            pltpu.VMEM((nx * nc, 8, hs), F32),
+            pltpu.VMEM((kvh, 8, hs), F32),
+            pltpu.VMEM((LATE, kvh, 8, hs), F32),
             pltpu.VMEM((nz, 8, hs), F32),
+            pltpu.VMEM((nz, LATE, 8, hs), F32),
             pltpu.VMEM((kvh, 8, hs), F32),
-            dma((2, kvh, HEADS_PER)), dma((kvh,)), dma((kvh,)), dma((3,)),
+            dma((kvh,)), dma((2,)), dma((kvh,)), dma((3,)),
             dma((2, kvh)), dma((2, kvh)), dma((2, kvh)), dma((2, kvh)), dma((kvh,)), dma((kvh,)),
             dma((kvh,)), dma((kvh,)), dma((kvh,)), dma((kvh,)),
-            dma((nx * nc,)), dma((nx * nc,)), dma((nz,)), dma((nz,)), dma((kvh,)), dma((kvh,)),
+            dma((kvh,)), dma((kvh,)), dma((LATE, kvh)), dma((LATE, kvh)),
+            dma((nz,)), dma((nz,)), dma((nz,)), dma((nz,)), dma((kvh,)), dma((kvh,)),
             dma((kvh, HEADS_PER + 2)),
         ],
         compiler_params=pltpu.CompilerParams(

time: 69.4 us -> 67.9 us (0.978); the launches traced: 69.2 us -> 66.8 us
  Pallas kernels: 68.6 us -> 66.2 us
    pallas_call x1, Pallas kernels: 67.3 us -> 64.9 us  [body(): pl.pallas_call(functools.partial(kernel, nx, nz, nc), out_shape=(jax.Shap...]
where the time goes in v3:
time: 67.9 us; the launch traced here: 66.8 us
  Pallas kernels  66.2 us (97%)
    pallas_call x1, Pallas kernels, body(): pl.pallas_call(functools.partial(kernel, nx, nz, nc), out_shape=(jax.Shap...  64.9 us

profile of v3, /device:TPU:33, one launch (start us, length us, event | category | flops | bytes accessed | tf_op | source)
XLA Modules:
  0.0 66.8 jit_solution(2212064829926342809)
XLA Ops:
  0.6 64.9 %shard_map.137 = (bf16[128,5120]{1,0:T(8,128)(2,1)S(1)}, bf16[128,1024]{1,0:T(8,128)(2,1)S(1)}, bf16[128,1024]{1,0:T(8,128)(2,1)S(1)}, f32[40,128]{1,0:T(8,128)S(1)}, f32[8,128]{1,0:T(8,128)S(1)}) custom-call(bf16[128,5120]{1,0:T(8,128)(2,1)} %q_hbm.1, bf16[128,1024]{1,0:T(8,128)(2,1)} %k_hbm.1, bf16[128,1024]{1,0:T(8,128)(2,1)} %v_hbm.1, ...), custom_call_target="tpu_custom_call" | custom-call | tf_op jit(solution)/shard_map/pallas_call | solution.py:588
  65.5 1.3 %shard_map.138 = (bf16[128,5120]{1,0:T(8,128)(2,1)}, bf16[128,1024]{1,0:T(8,128)(2,1)}, bf16[128,1024]{1,0:T(8,128)(2,1)}, f32[40,128]{1,0:T(8,128)}, f32[8,128]{1,0:T(8,128)}) custom-call(bf16[128,5120]{1,0:T(8,128)(2,1)S(1)} %get-tuple-element.15.refs_0_, bf16[128,1024]{1,0:T(8,128)(2,1)S(1)} %get-tuple-element.16.refs_1_, ...), custom_call_target="tpu_custom_call" | custom-call | tf_op jit(solution)/shard_map/pallas_call | solution.py:660

commit v4 on v3

--- a/solution.py
+++ b/solution.py
@@ -21,8 +21,6 @@
 QROWS = HEADS_PER * TOK
 CONTEXT = ("context_0", "context_1", "context_2")
 GROUPS_CONTEXT = ("groups", "context_0", "context_1", "context_2")
-LATE = 2
-EARLY = KEY_VALUE_HEADS - LATE
 NORM_EPS = 1e-06
 ROPE_BASE = 500000.0
 SCALE = HEAD_SIZE ** (-0.5)
@@ -55,11 +53,11 @@
     q_vm, g_vm, k_vm, kv, qr, st0, st1, dp0, dp1, pt, ds, dqw, dkw,
     bias, segcol, cosk, sink, cq, sq, rqb, rkb, inner,
     own, mid, sd, rd, si, ri, outb,
-    tops0, tops1, gpart, rs, pf, za, zf, ag,
+    tops0, tops1, gpart, rs, za, ag,
     in_sem, kin_sem, vin_sem, tab_sem,
     z_send, z_recv, c_send, c_recv, f_send, f_recv,
     d_send, d_recv, i_send, i_recv,
-    rs_send, rs_recv, pf_send, pf_recv, za_send, za_recv, zf_send, zf_recv, ag_send, ag_recv,
+    rs_send, rs_recv, za_send, za_recv, ag_send, ag_recv,
     out_sem,
 ):
     xi = lax.axis_index("context_0")
@@ -277,20 +275,6 @@
             device_id=rank_peer(source), device_id_type=MESH,
         )
 
-    def plane_out(late, d):
-        other = jnp.bitwise_xor(rank, d)
-        return pltpu.make_async_remote_copy(
-            gpart.at[EARLY + late], pf.at[late, rank], pf_send.at[late, d], pf_recv.at[late, rank],
-            device_id=rank_peer(other), device_id_type=MESH,
-        )
-
-    def plane_got(late, d):
-        other = jnp.bitwise_xor(rank, d)
-        return pltpu.make_async_remote_copy(
-            gpart.at[EARLY + late], pf.at[late, other], pf_send.at[late, d], pf_recv.at[late, other],
-            device_id=rank_peer(other), device_id_type=MESH,
-        )
-
     def z_copy(buffer, send, recv, d, source):
         return pltpu.make_async_remote_copy(
             buffer.at[source], buffer.at[source], send.at[d], recv.at[source],
@@ -303,12 +287,6 @@
     def z_got(d):
         return z_copy(za, za_send, za_recv, d, lax.rem(zi + d, nz))
 
-    def late_out(d):
-        return z_copy(zf, zf_send, zf_recv, d, zi)
-
-    def late_got(d):
-        return z_copy(zf, zf_send, zf_recv, d, lax.rem(zi + d, nz))
-
     def total_out(d):
         other = jnp.bitwise_xor(rank, d)
         return pltpu.make_async_remote_copy(
@@ -322,18 +300,15 @@
             device_id=rank_peer(source), device_id_type=MESH,
         )
 
-    far_first = sorted(range(1, nz), key=lambda d: -min(d, nz - d))
-    owner = rank < EARLY
+    near_first = sorted(range(1, nz), key=lambda d: min(d, nz - d))
 
     def shards_over_z():
-        @pl.when(owner)
-        def _():
-            rs[rank] = gpart[rank]
-            for d in range(1, nx * nc):
-                shard_got(jnp.bitwise_xor(rank, d)).wait_recv()
-            za[zi] = jnp.sum(rs[...], axis=0)
-            for d in far_first:
-                z_out(d).start()
+        rs[rank] = gpart[rank]
+        for d in range(1, nx * nc):
+            shard_got(jnp.bitwise_xor(rank, d)).wait_recv()
+        za[zi] = jnp.sum(rs[...], axis=0)
+        for d in near_first:
+            z_out(d).start()
 
     CH = 64
     nt = (((1,), (1,)), ((), ()))
@@ -440,13 +415,9 @@
                 softmax(j, slot)
         query_grads(h)
         key_grads(h)
-        if isinstance(h, int):
-            for d in range(1, nx * nc):
-                plane_out(h - EARLY, d).start()
-        else:
-            @pl.when(rank != h)
-            def _():
-                shard_out(h).start()
+        @pl.when(rank != h)
+        def _():
+            shard_out(h).start()
 
         grads_to_partner(h).start()
 
@@ -455,24 +426,18 @@
     arrived(0)
     scores(0, 0)
 
-    @pl.loop(0, EARLY // 2)
+    last = KEY_VALUE_HEADS - 1
+
+    @pl.loop(0, last // 2)
     def _(i):
         step(2 * i, 0, first=i == 0)
         step(2 * i + 1, 1, first=i == 0)
 
-    last = KEY_VALUE_HEADS - 1
     step(last - 1, 0)
     step(last, 1, last=True)
     add_and_send(last - 1)
     shards_over_z()
 
-    for late in range(LATE):
-        pf[late, rank] = gpart[EARLY + late]
-        for d in range(1, nx * nc):
-            plane_got(late, d).wait_recv()
-        zf[zi, late] = jnp.sum(pf[late], axis=0)
-    for d in far_first:
-        late_out(d).start()
     add_and_send(last)
 
     inner_q = jnp.sum(inner[...], axis=1, keepdims=True) * (1.0 / (QUERY_HEADS * HEAD_SIZE))
@@ -493,13 +458,11 @@
             outb[h, rows] = (rqb[...] * weighted - x * inner[...]).astype(BF16)
             q_out(h, j).start()
 
-    @pl.when(owner)
-    def _():
-        for d in range(1, nz):
-            z_got(d).wait_recv()
-        ag[rank] = jnp.sum(za[...], axis=0)
-        for d in range(1, nx * nc):
-            total_out(d).start()
+    for d in range(1, nz):
+        z_got(d).wait_recv()
+    ag[rank] = jnp.sum(za[...], axis=0)
+    for d in range(1, nx * nc):
+        total_out(d).start()
 
     def k_out(h, s, out):
         cols = pl.ds(pl.multiple_of(h * HEAD_SIZE, HEAD_SIZE), HEAD_SIZE)
@@ -526,17 +489,13 @@
         si[h, 0] = (rkb[...] * dkw[h] - k_vm[h].astype(F32) * inner[...]).astype(BF16)
         k_out(h, 0, kgrad_hbm).start()
 
-    for d in range(1, nz):
-        late_got(d).wait_recv()
-    late_totals = jnp.sum(zf[...], axis=0)
-    for source in range(EARLY):
+    for source in range(KEY_VALUE_HEADS):
         @pl.when(rank != source)
         def _():
             total_got(source).wait_recv()
-    for h in range(KEY_VALUE_HEADS):
-        total = ag[h] if h < EARLY else late_totals[h - EARLY]
-        qgain_ref[h * HEADS_PER : (h + 1) * HEADS_PER, :] = total[0:HEADS_PER, :]
-        kgain_ref[h : h + 1, :] = total[HEADS_PER : HEADS_PER + 1, :]
+
+        qgain_ref[source * HEADS_PER : (source + 1) * HEADS_PER, :] = ag[source, 0:HEADS_PER, :]
+        kgain_ref[source : source + 1, :] = ag[source, HEADS_PER : HEADS_PER + 1, :]
 
     @pl.loop(0, KEY_VALUE_HEADS)
     def _(h):
@@ -550,22 +509,14 @@
         k_out(h, 0, kgrad_hbm).wait()
         k_out(h, 1, vgrad_hbm).wait()
 
-    for h in range(EARLY):
+    for h in range(KEY_VALUE_HEADS):
         @pl.when(rank != h)
         def _():
             shard_out(h).wait_send()
     for d in range(1, nx * nc):
-        for late in range(LATE):
-            plane_out(late, d).wait_send()
+        total_out(d).wait_send()
     for d in range(1, nz):
-        late_out(d).wait_send()
-
-    @pl.when(owner)
-    def _():
-        for d in range(1, nx * nc):
-            total_out(d).wait_send()
-        for d in range(1, nz):
-            z_out(d).wait_send()
+        z_out(d).wait_send()
 
 
 def settle(*refs):
@@ -633,15 +584,12 @@
             pltpu.VMEM((8, TOK), F32),
             pltpu.VMEM((kvh, 8, hs), F32),
             pltpu.VMEM((kvh, 8, hs), F32),
-            pltpu.VMEM((LATE, kvh, 8, hs), F32),
             pltpu.VMEM((nz, 8, hs), F32),
-            pltpu.VMEM((nz, LATE, 8, hs), F32),
             pltpu.VMEM((kvh, 8, hs), F32),
             dma((kvh,)), dma((2,)), dma((kvh,)), dma((3,)),
             dma((2, kvh)), dma((2, kvh)), dma((2, kvh)), dma((2, kvh)), dma((kvh,)), dma((kvh,)),
             dma((kvh,)), dma((kvh,)), dma((kvh,)), dma((kvh,)),
-            dma((kvh,)), dma((kvh,)), dma((LATE, kvh)), dma((LATE, kvh)),
-            dma((nz,)), dma((nz,)), dma((nz,)), dma((nz,)), dma((kvh,)), dma((kvh,)),
+            dma((kvh,)), dma((kvh,)), dma((nz,)), dma((nz,)), dma((kvh,)), dma((kvh,)),
             dma((kvh, HEADS_PER + 2)),
         ],
         compiler_params=pltpu.CompilerParams(

time: 67.9 us -> 67 us (0.987); the launches traced: 66.8 us -> 66.8 us
  no operation moved by 1% of the time
where the time goes in v4:
time: 67 us; the launch traced here: 66.8 us
  Pallas kernels  66.2 us (99%)
    pallas_call x1, Pallas kernels, body(): pl.pallas_call(functools.partial(kernel, nx, nz, nc), out_shape=(jax.Shap...  64.9 us

profile of v4, /device:TPU:33, one launch (start us, length us, event | category | flops | bytes accessed | tf_op | source)
XLA Modules:
  0.0 66.8 jit_solution(11481128955984559102)
XLA Ops:
  0.6 64.9 %shard_map.137 = (bf16[128,5120]{1,0:T(8,128)(2,1)S(1)}, bf16[128,1024]{1,0:T(8,128)(2,1)S(1)}, bf16[128,1024]{1,0:T(8,128)(2,1)S(1)}, f32[40,128]{1,0:T(8,128)S(1)}, f32[8,128]{1,0:T(8,128)S(1)}) custom-call(bf16[128,5120]{1,0:T(8,128)(2,1)} %q_hbm.1, bf16[128,1024]{1,0:T(8,128)(2,1)} %k_hbm.1, bf16[128,1024]{1,0:T(8,128)(2,1)} %v_hbm.1, ...), custom_call_target="tpu_custom_call" | custom-call | tf_op jit(solution)/shard_map/pallas_call | solution.py:539
  65.6 1.3 %shard_map.138 = (bf16[128,5120]{1,0:T(8,128)(2,1)}, bf16[128,1024]{1,0:T(8,128)(2,1)}, bf16[128,1024]{1,0:T(8,128)(2,1)}, f32[40,128]{1,0:T(8,128)}, f32[8,128]{1,0:T(8,128)}) custom-call(bf16[128,5120]{1,0:T(8,128)(2,1)S(1)} %get-tuple-element.15.refs_0_, bf16[128,1024]{1,0:T(8,128)(2,1)S(1)} %get-tuple-element.16.refs_1_, ...), custom_call_target="tpu_custom_call" | custom-call | tf_op jit(solution)/shard_map/pallas_call | solution.py:608

commit v5 on v4

--- a/solution.py
+++ b/solution.py
@@ -57,7 +57,7 @@
     in_sem, kin_sem, vin_sem, tab_sem,
     z_send, z_recv, c_send, c_recv, f_send, f_recv,
     d_send, d_recv, i_send, i_recv,
-    rs_send, rs_recv, za_send, za_recv, ag_send, ag_recv,
+    rs_send, rs_recv, za_send, za_recv, ag_send, ag_recv, near_sem,
     out_sem,
 ):
     xi = lax.axis_index("context_0")
@@ -107,10 +107,25 @@
         pl.semaphore_signal(
             barrier, inc=1, device_id=rank_peer(jnp.bitwise_xor(rank, d)), device_id_type=MESH
         )
-    for d in range(1, nz):
+    sides = sorted({1, nz - 1})
+    for d in sides:
         pl.semaphore_signal(
             barrier, inc=1, device_id={"context_1": lax.rem(zi + d, nz)}, device_id_type=MESH
         )
+
+    rounds = [1 << r for r in range(8) if 1 << r < nz // 2]
+
+    def tell(r):
+        for side, d in enumerate((rounds[r], nz - rounds[r])):
+            pl.semaphore_signal(
+                near_sem.at[r, side], inc=1,
+                device_id={"context_1": lax.rem(zi + d, nz)}, device_id_type=MESH,
+            )
+
+    def heard(r):
+        for side in range(2):
+            pl.semaphore_wait(near_sem.at[r, side], 1)
+
 
     my_local = 2 * lax.rem(zi, 2) + ci
     sub_iota = lax.broadcasted_iota(jnp.int32, (SPAN, TOK), 0)
@@ -170,7 +185,9 @@
         to_partner(1, h).start()
 
     AHEAD = 2
-    pl.semaphore_wait(barrier, nx * nc - 1 + nz - 1)
+    pl.semaphore_wait(barrier, nx * nc - 1 + len(sides))
+    if rounds:
+        tell(0)
     for h in range(AHEAD):
         values_out(h)
 
@@ -307,6 +324,8 @@
         for d in range(1, nx * nc):
             shard_got(jnp.bitwise_xor(rank, d)).wait_recv()
         za[zi] = jnp.sum(rs[...], axis=0)
+        if rounds:
+            heard(len(rounds) - 1)
         for d in near_first:
             z_out(d).start()
 
@@ -430,6 +449,12 @@
 
     @pl.loop(0, last // 2)
     def _(i):
+        for r in range(1, len(rounds)):
+            @pl.when(i == r)
+            def _():
+                heard(r - 1)
+                tell(r)
+
         step(2 * i, 0, first=i == 0)
         step(2 * i + 1, 1, first=i == 0)
 
@@ -590,6 +615,7 @@
             dma((2, kvh)), dma((2, kvh)), dma((2, kvh)), dma((2, kvh)), dma((kvh,)), dma((kvh,)),
             dma((kvh,)), dma((kvh,)), dma((kvh,)), dma((kvh,)),
             dma((kvh,)), dma((kvh,)), dma((nz,)), dma((nz,)), dma((kvh,)), dma((kvh,)),
+            pltpu.SemaphoreType.REGULAR((3, 2)),
             dma((kvh, HEADS_PER + 2)),
         ],
         compiler_params=pltpu.CompilerParams(

time: 67 us -> 61.8 us (0.922)
  Pallas kernels: 66.2 us -> 61 us
    pallas_call x1, Pallas kernels: 64.9 us -> 59.7 us  [body(): pl.pallas_call(functools.partial(kernel, nx, nz, nc), out_shape=(jax.Shap...]
where the time goes in v5:
time: 61.8 us; the launch traced here: 61.6 us
  Pallas kernels  61 us (99%)
  between operations  0.64 us (1%)
    pallas_call x1, Pallas kernels, body(): pl.pallas_call(functools.partial(kernel, nx, nz, nc), out_shape=(jax.Shap...  59.7 us
    pallas_call x1, Pallas kernels, body(): pl.pallas_call(settle, out_shape=[jax.ShapeDtypeStruct(o.shape, o.dtype)...  1.27 us

profile of v5, /device:TPU:33, one launch (start us, length us, event | category | flops | bytes accessed | tf_op | source)
XLA Modules:
  0.0 61.6 jit_solution(6142543243542186462)
XLA Ops:
  0.6 59.7 %shard_map.137 = (bf16[128,5120]{1,0:T(8,128)(2,1)S(1)}, bf16[128,1024]{1,0:T(8,128)(2,1)S(1)}, bf16[128,1024]{1,0:T(8,128)(2,1)S(1)}, f32[40,128]{1,0:T(8,128)S(1)}, f32[8,128]{1,0:T(8,128)S(1)}) custom-call(bf16[128,5120]{1,0:T(8,128)(2,1)} %q_hbm.1, bf16[128,1024]{1,0:T(8,128)(2,1)} %k_hbm.1, bf16[128,1024]{1,0:T(8,128)(2,1)} %v_hbm.1, ...), custom_call_target="tpu_custom_call" | custom-call | tf_op jit(solution)/shard_map/pallas_call | solution.py:564
  60.3 1.3 %shard_map.138 = (bf16[128,5120]{1,0:T(8,128)(2,1)}, bf16[128,1024]{1,0:T(8,128)(2,1)}, bf16[128,1024]{1,0:T(8,128)(2,1)}, f32[40,128]{1,0:T(8,128)}, f32[8,128]{1,0:T(8,128)}) custom-call(bf16[128,5120]{1,0:T(8,128)(2,1)S(1)} %get-tuple-element.15.refs_0_, bf16[128,1024]{1,0:T(8,128)(2,1)S(1)} %get-tuple-element.16.refs_1_, ...), custom_call_target="tpu_custom_call" | custom-call | tf_op jit(solution)/shard_map/pallas_call | solution.py:634

commit v6 on v5

--- a/solution.py
+++ b/solution.py
@@ -265,6 +265,8 @@
         to_across(1, h).wait_recv()
         forward(h).start()
 
+    take(0)
+
     @pl.loop(0, KEY_VALUE_HEADS)
     def _(h):
         for j in range(HEADS_PER):
@@ -440,8 +442,7 @@
 
         grads_to_partner(h).start()
 
-    for h in range(2):
-        take(h)
+    take(1)
     arrived(0)
     scores(0, 0)
 

time: 61.8 us -> 61.8 us (level)
  no operation moved by 1% of the time
where the time goes in v6:
time: 61.8 us; the launch traced here: 61.6 us
  Pallas kernels  61 us (99%)
  between operations  0.64 us (1%)
    pallas_call x1, Pallas kernels, body(): pl.pallas_call(functools.partial(kernel, nx, nz, nc), out_shape=(jax.Shap...  59.7 us
    pallas_call x1, Pallas kernels, body(): pl.pallas_call(settle, out_shape=[jax.ShapeDtypeStruct(o.shape, o.dtype)...  1.27 us

profile of v6, /device:TPU:33, one launch (start us, length us, event | category | flops | bytes accessed | tf_op | source)
XLA Modules:
  0.0 61.6 jit_solution(16612122580066497621)
XLA Ops:
  0.6 59.7 %shard_map.137 = (bf16[128,5120]{1,0:T(8,128)(2,1)S(1)}, bf16[128,1024]{1,0:T(8,128)(2,1)S(1)}, bf16[128,1024]{1,0:T(8,128)(2,1)S(1)}, f32[40,128]{1,0:T(8,128)S(1)}, f32[8,128]{1,0:T(8,128)S(1)}) custom-call(bf16[128,5120]{1,0:T(8,128)(2,1)} %q_hbm.1, bf16[128,1024]{1,0:T(8,128)(2,1)} %k_hbm.1, bf16[128,1024]{1,0:T(8,128)(2,1)} %v_hbm.1, ...), custom_call_target="tpu_custom_call" | custom-call | tf_op jit(solution)/shard_map/pallas_call | solution.py:565
  60.3 1.3 %shard_map.138 = (bf16[128,5120]{1,0:T(8,128)(2,1)}, bf16[128,1024]{1,0:T(8,128)(2,1)}, bf16[128,1024]{1,0:T(8,128)(2,1)}, f32[40,128]{1,0:T(8,128)}, f32[8,128]{1,0:T(8,128)}) custom-call(bf16[128,5120]{1,0:T(8,128)(2,1)S(1)} %get-tuple-element.15.refs_0_, bf16[128,1024]{1,0:T(8,128)(2,1)S(1)} %get-tuple-element.16.refs_1_, ...), custom_call_target="tpu_custom_call" | custom-call | tf_op jit(solution)/shard_map/pallas_call | solution.py:635
